TPU v7x, 32 devices: a whole 2x2x4 slice. The times are simulated.
32 devices in a mesh: atoms: 8 (over z, x), modes: 4 (over y, core).
Axes of the slice: x: 2, y: 2, z: 4, core: 2. Of those that a mesh axis runs over, the one named last changes fastest.
Arguments:
- subspace: float32 [768, 16384], P('modes', 'atoms'), may hold values from -100 to 100
- applied: float32 [768, 16384], P('modes', 'atoms'), may hold values from -300 to 300
Outputs:
- ortho_basis: float32 [768, 16384], P('modes', 'atoms')
- projected: float32 [768, 768], P('modes')
All inputs are finite; a program needn't handle non-finite values.
Results may differ from a plain program's by a relative error of at most 0.00025.
Values sent between devices are 32-bit elements; how exact they have to be, the bound alone decides.
No kernel may reach another device: no remote copies, remote signals or barrier semaphores. Data moves between devices by JAX's collectives and lax.ppermute only.
A program may use at most 64 MiB of HBM per device.

v0:
```python
import jax
import jax.numpy as jnp
from jax import lax
from jax.sharding import PartitionSpec as P


def contract_cols(left, right):
    return lax.dot_general(
        left,
        right,
        (((1,), (1,)), ((), ())),
        precision=lax.Precision.HIGHEST,
        preferred_element_type=jnp.float32,
    )


def matmul(left, right):
    return jnp.dot(left, right, precision=lax.Precision.HIGHEST, preferred_element_type=jnp.float32)


def inverses(gram_full):
    factor = jnp.linalg.cholesky(gram_full)
    identity = jnp.eye(gram_full.shape[0], dtype=gram_full.dtype)
    inv_lower = lax.linalg.triangular_solve(factor, identity, left_side=True, lower=True)
    return (inv_lower, inv_lower.T)


def per_device(subspace, applied):
    mode_width = subspace.shape[0]
    row_total = subspace.shape[1] * lax.axis_size("atoms")
    mode_start = lax.axis_index("modes") * mode_width
    full_modes = lax.all_gather(subspace, "modes", axis=0, tiled=True)
    gram_part = contract_cols(subspace, full_modes) / row_total
    crosst_part = contract_cols(applied, full_modes) / row_total
    gram_rows, crosst_rows = lax.psum((gram_part, crosst_part), "atoms")
    gram_full, crosst_full = (
        lax.all_gather(gram_rows, "modes", axis=0, tiled=True),
        lax.all_gather(crosst_rows, "modes", axis=0, tiled=True),
    )
    inv_lower, inv_upper = inverses(gram_full)
    lower_rows = lax.dynamic_slice_in_dim(inv_lower, mode_start, mode_width, 0)
    ortho_basis = matmul(lower_rows, full_modes)
    projected = matmul(matmul(lower_rows, crosst_full.T), inv_upper)
    return (ortho_basis, projected)


def solution(mesh):
    return jax.shard_map(
        per_device,
        mesh=mesh,
        in_specs=(P("modes", "atoms"), P("modes", "atoms")),
        out_specs=(P("modes", "atoms"), P("modes", None)),
        check_vma=False,
    )
```

profile of v0, /device:TPU:0, one launch (start us, length us, event | category | flops | bytes accessed | tf_op | source)
XLA Modules:
  0.0 456.1 jit_solution(12077088014024329457)
XLA Ops:
  8.0 50.7 %all-gather.4.cloned.1.call-done = f32[768,2048]{1,0:T(8,128)} async-done(((f32[192,2048]{1,0:T(8,128)}), f32[768,2048]{1,0:T(8,128)}) %all-gather.4.cloned.1.call-update) | async-done | bytes 6291472 | tf_op jit(solution)/shard_map/all_gather | solution.py:32
  58.7 9.4 %convolution_multiply_fusion.1 = f32[192,768]{1,0:T(8,128)} fusion(f32[192,2048]{1,0:T(8,128)S(1)} %copy-done.3, f32[768,2048]{1,0:T(8,128)} %all-gather.4.cloned.1.call-done), kind=kOutput, calls=%fused_computation.17 | convolution fusion | flops 3624026112 | bytes 8454144 | tf_op jit(solution)/shard_map/dot_general | solution.py:8
  68.1 7.2 %convolution_multiply_fusion = f32[192,768]{1,0:T(8,128)} fusion(f32[192,2048]{1,0:T(8,128)S(1)} %copy-done, f32[768,2048]{1,0:T(8,128)S(1)} %copy-done.1), kind=kOutput, calls=%fused_computation.15 | convolution fusion | flops 3624026112 | bytes 8454144 | tf_op jit(solution)/shard_map/dot_general | solution.py:8
  75.3 80.4 %all-reduce.4.cloned.1.call-done = (f32[192,768]{1,0:T(8,128)}, f32[192,768]{1,0:T(8,128)}) async-done(((f32[192,768]{1,0:T(8,128)}, f32[192,768]{1,0:T(8,128)}), (f32[192,768]{1,0:T(8,128)}, f32[192,768]{1,0:T(8,128)})) %all-reduce.4.cloned.1.call-update) | async-done | bytes 1179664 | tf_op jit(solution)/shard_map/psum | solution.py:35
  157.7 22.9 %all-gather.6.cloned.1.call-done = f32[768,768]{1,0:T(8,128)} async-done(((f32[192,768]{1,0:T(8,128)}), f32[768,768]{1,0:T(8,128)}) %all-gather.6.cloned.1.call-update) | async-done | bytes 2359312 | tf_op jit(solution)/shard_map/all_gather | solution.py:37
  180.6 3.2 copy.6
  183.8 2.7 fusion
  188.0 11.7 %cholesky.165 = f32[128,128]{1,0:T(8,128)S(1)} custom-call(f32[128,128]{1,0:T(8,128)S(1)} %cholesky.424), custom_call_target="Cholesky" | custom-call | tf_op jit(solution)/shard_map/jit(cholesky)/cholesky | solution.py:22
  199.7 9.8 %custom-call.46 = f32[1,128,128]{1,2,0:T(8,128)S(1)} custom-call(f32[1,128,128]{2,1,0:T(8,128)S(1)} %get-tuple-element.47), custom_call_target="InvertDiagBlocksLowerTriangular" | custom-call | tf_op jit(solution)/shard_map/jit(cholesky)/cholesky | solution.py:22
  214.6 11.7 %cholesky.188 = f32[128,128]{1,0:T(8,128)S(1)} custom-call(f32[128,128]{1,0:T(8,128)S(1)} %cholesky.428), custom_call_target="Cholesky" | custom-call | tf_op jit(solution)/shard_map/jit(cholesky)/cholesky | solution.py:22
  227.0 10.2 %custom-call.47 = f32[1,128,128]{1,2,0:T(8,128)S(1)} custom-call(f32[1,128,128]{2,1,0:T(8,128)S(1)} %get-tuple-element.44), custom_call_target="InvertDiagBlocksLowerTriangular" | custom-call | tf_op jit(solution)/shard_map/jit(cholesky)/cholesky | solution.py:22
  240.1 11.7 %cholesky.354 = f32[128,128]{1,0:T(8,128)S(1)} custom-call(f32[128,128]{1,0:T(8,128)S(1)} %cholesky.433), custom_call_target="Cholesky" | custom-call | tf_op jit(solution)/shard_map/jit(cholesky)/cholesky | solution.py:22
  253.1 9.8 %custom-call.48 = f32[1,128,128]{1,2,0:T(8,128)S(1)} custom-call(f32[1,128,128]{2,1,0:T(8,128)S(1)} %get-tuple-element.41), custom_call_target="InvertDiagBlocksLowerTriangular" | custom-call | tf_op jit(solution)/shard_map/jit(cholesky)/cholesky | solution.py:22
  265.8 11.9 %cholesky.373 = f32[128,128]{1,0:T(8,128)S(1)} custom-call(f32[128,128]{1,0:T(8,128)S(1)} %cholesky.438), custom_call_target="Cholesky" | custom-call | tf_op jit(solution)/shard_map/jit(cholesky)/cholesky | solution.py:22
  279.0 9.8 %custom-call.49 = f32[1,128,128]{1,2,0:T(8,128)S(1)} custom-call(f32[1,128,128]{2,1,0:T(8,128)S(1)} %get-tuple-element.38), custom_call_target="InvertDiagBlocksLowerTriangular" | custom-call | tf_op jit(solution)/shard_map/jit(cholesky)/cholesky | solution.py:22
  291.5 11.7 %cholesky.392 = f32[128,128]{1,0:T(8,128)S(1)} custom-call(f32[128,128]{1,0:T(8,128)S(1)} %cholesky.443), custom_call_target="Cholesky" | custom-call | tf_op jit(solution)/shard_map/jit(cholesky)/cholesky | solution.py:22
  304.6 9.8 %custom-call.50 = f32[1,128,128]{1,2,0:T(8,128)S(1)} custom-call(f32[1,128,128]{2,1,0:T(8,128)S(1)} %get-tuple-element.35), custom_call_target="InvertDiagBlocksLowerTriangular" | custom-call | tf_op jit(solution)/shard_map/jit(cholesky)/cholesky | solution.py:22
  316.9 11.9 %cholesky.410 = f32[128,128]{1,0:T(8,128)S(1)} custom-call(f32[128,128]{1,0:T(8,128)S(1)} %convolution_subtract_fusion.8), custom_call_target="Cholesky" | custom-call | tf_op jit(solution)/shard_map/jit(cholesky)/cholesky | solution.py:22
  334.4 3.3 select_select_fusion
  337.8 17.9 %while.1 = (s32[]{:T(128)}, f32[768,768]{1,0:T(8,128)}, s32[6,2]{0,1:T(2,128)S(1)}, f32[6,128,128]{2,1,0:T(8,128)S(1)}, s32[]{:T(128)}) while((s32[]{:T(128)}, f32[768,768]{1,0:T(8,128)}, s32[6,2]{0,1:T(2,128)S(1)}, f32[6,128,128]{2,1,0:T(8,128)S(1)}, s32[]{:T(128)}) %tuple.44), condition=%wide.while_cond, body=%wide.while_body.sunk | while | flops 2 | bytes 131181 | solution.py:24
  355.6 59.0 %custom-call.51 = f32[6,128,128]{1,2,0:T(8,128)S(1)} custom-call(f32[6,128,128]{2,1,0:T(8,128)S(1)} %get-tuple-element.9), custom_call_target="InvertDiagBlocksLowerTriangular" | custom-call | tf_op jit(solution)/shard_map/triangular_solve | solution.py:24
  431.3 4.3 fusion.22
  435.6 4.9 %fusion.61 = f32[192,768]{1,0:T(8,128)} fusion(f32[192,768]{1,0:T(8,128)S(1)} %fusion.22, f32[768,768]{1,0:T(8,128)} %convolution_dynamic-update-slice_fusion), kind=kOutput, calls=%fused_computation.123 | convolution fusion | flops 1358954496 | bytes 3538944 | tf_op jit(solution)/shard_map/dot_general | solution.py:18
  440.5 8.7 %fusion.24 = f32[192,2048]{1,0:T(8,128)} fusion(f32[768,2048]{1,0:T(8,128)} %all-gather.4.cloned.1.call-done, f32[768,768]{1,0:T(8,128)} %convolution_dynamic-update-slice_fusion, s32[]{:T(128)S(6)} %select_n.8), kind=kOutput, calls=%fused_computation.44 | convolution fusion | flops 3623878656 | bytes 8454148 | tf_op jit(solution)/shard_map/dot_general | solution.py:18
  (80 shorter events, 61.1 us)
Async XLA Ops:
  7.2 60.9 %copy-start = (f32[192,2048]{1,0:T(8,128)S(1)}, f32[192,2048]{1,0:T(8,128)}, u32[]{:S(2)}) copy-start(f32[192,2048]{1,0:T(8,128)} %param.3) | copy-start | bytes 4718596
  7.2 51.5 %copy-start.3 = (f32[192,2048]{1,0:T(8,128)S(1)}, f32[192,2048]{1,0:T(8,128)}, u32[]{:S(2)}) copy-start(f32[192,2048]{1,0:T(8,128)} %param.2) | copy-start | bytes 4718596
  7.2 51.5 %all-gather.4.cloned.1.call-start = ((), (), s32[]{:S(2)}) async-start(), calls=%async_computation | async-start | bytes 7864320 | tf_op jit(solution)/shard_map/all_gather | solution.py:32
  7.9 147.9 %all-reduce.4.cloned.1.call-start = ((), (), s32[]{:S(2)}) async-start(), calls=%async_computation.3 | async-start | bytes 2359296 | tf_op jit(solution)/shard_map/psum | solution.py:35
  58.7 9.4 %copy-start.1 = (f32[768,2048]{1,0:T(8,128)S(1)}, f32[768,2048]{1,0:T(8,128)}, u32[]{:S(2)}) copy-start(f32[768,2048]{1,0:T(8,128)} %all-gather.4.cloned.1.call-done) | copy-start | bytes 18874372
  75.3 105.3 %all-gather.6.cloned.1.call-start = ((), (), s32[]{:S(2)}) async-start(), calls=%async_computation.1 | async-start | bytes 2949120 | tf_op jit(solution)/shard_map/all_gather | solution.py:37
  155.8 275.5 %all-gather.8.cloned.1.call-start = ((), (), s32[]{:S(2)}) async-start(), calls=%async_computation.2 | async-start | bytes 2949120 | tf_op jit(solution)/shard_map/all_gather | solution.py:38
  186.5 1.5 copy-start.4
  414.6 4.0 copy-start.2
Sparse Core Ops, SparseCore 0:
  9.6 49.0 all-gather.3
  75.4 80.3 all-reduce.3
  157.3 23.2 all-gather.5
  182.0 24.1 all-gather.7
where the time goes:
time: 464 us; the launch traced here: 456 us
  other arithmetic  193 us (42%)
  waiting for transfers between devices  155 us (33%)
  matrix products  65.5 us (14%)
  local copies, waits for them, and re-layouts  24.1 us (5%)
  between operations  18.2 us (4%)
    another operation x22, other arithmetic, inverses(): factor = jnp.linalg.cholesky(gram_full)  127 us
    psum x1, waiting for transfers between devices, per_device(): gram_rows, crosst_rows = lax.psum((gram_part, crosst_part), 'atoms')  80.4 us
    another operation x3, other arithmetic, inverses(): lax.linalg.triangular_solve(factor, identity, left_side=True, lower=True)  62.3 us
    all_gather x1, waiting for transfers between devices, per_device(): full_modes = lax.all_gather(subspace, 'modes', axis=0, tiled=True)  50.7 us
    all_gather x1, waiting for transfers between devices, per_device(): lax.all_gather(gram_rows, 'modes', axis=0, tiled=True)  22.9 us
    dot_general x3, matrix products, matmul(): jnp.dot(left, right, precision=lax.Precision.HIGHEST, preferred_element_t...  17.9 us
    another operation x18, local copies, waits for them, and re-layouts  17.8 us
    another operation x11, matrix products, inverses(): lax.linalg.triangular_solve(factor, identity, left_side=True, lower=True)  16.6 us
  transfers between devices with their start and end apart: 4, of which 3 were waited for; matrix products, arithmetic and copies ran while one was open for 54% of the time, Pallas kernels for 0%

commit v1 on v0

v1 whole, which is shorter than its diff:
```python
import jax
import jax.numpy as jnp
from jax import lax
from jax.experimental import pallas as pl
from jax.experimental.pallas import tpu as pltpu
from jax.sharding import PartitionSpec as P

LANES = 128
SUB = 32
PREC = lax.Precision.HIGHEST


def mm(a, b, prec=None):
    return lax.dot_general(a, b, (((1,), (0,)), ((), ())), precision=prec or PREC, preferred_element_type=jnp.float32)


def base_factor(w, s):
    lane = lax.broadcasted_iota(jnp.int32, (SUB, LANES), 1)
    row = lax.broadcasted_iota(jnp.int32, (SUB, LANES), 0)
    cols = [jnp.broadcast_to(w[:, SUB * s + k : SUB * s + k + 1], (SUB, LANES)) for k in range(SUB)]
    in_block = (lane >= SUB * s) & (lane < SUB * (s + 1))
    w = jnp.where(in_block, (lane - SUB * s == row).astype(jnp.float32), w)
    scale = jnp.ones((SUB, LANES), jnp.float32)
    for k in range(SUB):
        g = (k // 8) * 8
        r = k - g
        rows = SUB - g
        live = row[:rows] > r
        pivot = jnp.broadcast_to(cols[k][r : r + 1], (rows, LANES))
        scale_new = lax.rsqrt(pivot)
        inv = 1.0 / pivot[:8]
        inv = jnp.broadcast_to(inv[:1], (rows, LANES)) if rows > 8 else inv
        c = jnp.where(live, cols[k] * inv, 0.0)
        scale = jnp.concatenate([scale[:g], jnp.where(row[:rows] == r, scale_new, scale[g:])], 0) if g else jnp.where(row == r, scale_new, scale)
        drop = 8 if r == 7 else 0
        for m in range(k + 1, SUB):
            cols[m] = (cols[m] - c * jnp.broadcast_to(cols[m][r : r + 1], (rows, LANES)))[drop:]
        tail = w[g:] - c * jnp.broadcast_to(w[k : k + 1], (rows, LANES))
        w = jnp.concatenate([w[:g], tail], 0) if g else tail
    return w * scale


def diag_factor(a):
    n = LANES // SUB
    blocks = [a[SUB * t : SUB * (t + 1)] for t in range(n)]
    lane = lax.broadcasted_iota(jnp.int32, (SUB, LANES), 1)
    for s in range(n):
        blocks[s] = base_factor(blocks[s], s)
        if s + 1 < n:
            coef = jnp.transpose(blocks[s])[SUB * (s + 1) :]
            delta = mm(coef, blocks[s])
            keep = (lane < SUB * s) | (lane >= SUB * (s + 1))
            for t in range(s + 1, n):
                blocks[t] = jnp.where(keep, blocks[t], 0.0) - delta[SUB * (t - s - 1) : SUB * (t - s)]
    full = jnp.concatenate(blocks, 0)
    r = lax.broadcasted_iota(jnp.int32, (LANES, LANES), 0)
    c = lax.broadcasted_iota(jnp.int32, (LANES, LANES), 1)
    return jnp.where(c <= r, full, 0.0)


def inverse_kernel(g_ref, x_ref):
    size = g_ref.shape[0]
    n = size // LANES
    x_ref[...] = g_ref[...]

    def at(t):
        return pl.ds(pl.multiple_of(t * LANES, LANES), LANES)

    def step(p, _):
        x = diag_factor(x_ref[at(p), at(p)])
        panel = mm(x, x_ref[at(p), :])
        x_ref[at(p), :] = panel
        x_ref[at(p), at(p)] = x

        def trailing(t, _):
            coef = jnp.transpose(x_ref[at(p), at(t)])
            x_ref[at(t), at(p)] = jnp.zeros((LANES, LANES), jnp.float32)
            x_ref[at(t), :] = x_ref[at(t), :] - mm(coef, x_ref[at(p), :])
            return 0

        lax.fori_loop(p + 1, n, trailing, 0)
        return 0

    lax.fori_loop(0, n, step, 0)
    for t in range(n - 1):
        x_ref[LANES * t : LANES * (t + 1), LANES * (t + 1) :] = jnp.zeros((LANES, size - LANES * (t + 1)), jnp.float32)


def cholesky_inverse(gram):
    return pl.pallas_call(
        inverse_kernel,
        out_shape=jax.ShapeDtypeStruct(gram.shape, jnp.float32),
        in_specs=[pl.BlockSpec(memory_space=pltpu.VMEM)],
        out_specs=pl.BlockSpec(memory_space=pltpu.VMEM),
        cost_estimate=pl.CostEstimate(flops=50_000_000_000, bytes_accessed=4_000_000, transcendentals=0),
    )(gram)


def contract_cols(left, right):
    return lax.dot_general(
        left, right, (((1,), (1,)), ((), ())), precision=lax.Precision.HIGH, preferred_element_type=jnp.float32
    )


def per_device(subspace, applied):
    mode_width = subspace.shape[0]
    row_total = subspace.shape[1] * lax.axis_size("atoms")
    mode_start = lax.axis_index("modes") * mode_width
    full_modes = lax.all_gather(subspace, "modes", axis=0, tiled=True)
    gram_part = contract_cols(subspace, full_modes) / row_total
    crosst_part = contract_cols(applied, full_modes) / row_total
    gram_rows, crosst_rows = lax.psum((gram_part, crosst_part), "atoms")
    gram_full = lax.all_gather(gram_rows, "modes", axis=0, tiled=True)
    crosst_full = lax.all_gather(crosst_rows, "modes", axis=0, tiled=True)
    inv_lower = cholesky_inverse(gram_full)
    lower_rows = lax.dynamic_slice_in_dim(inv_lower, mode_start, mode_width, 0)
    high = lax.Precision.HIGH
    ortho_basis = mm(lower_rows, full_modes, high)
    projected = contract_cols(contract_cols(lower_rows, crosst_full), inv_lower)
    return (ortho_basis, projected)


def solution(mesh):
    return jax.shard_map(
        per_device,
        mesh=mesh,
        in_specs=(P("modes", "atoms"), P("modes", "atoms")),
        out_specs=(P("modes", "atoms"), P("modes", None)),
        check_vma=False,
    )
```

time: 464 us -> 232 us (0.50); the launches traced: 456 us -> 231 us
  other arithmetic: 193 us -> 0 us
  matrix products: 65.5 us -> 23 us
  Pallas kernels: 0 us -> 37.9 us
  local copies, waits for them, and re-layouts: 24.1 us -> 0.02 us
    another operation x25 -> x0, other arithmetic: 189 us -> none  [the longest x22 127 us: inverses(): factor = jnp.linalg.cholesky(gram_full)]
    pallas_call x0 -> x1, Pallas kernels: none -> 37.9 us  [cholesky_inverse(): pl.pallas_call(inverse_kernel, out_shape=jax.ShapeDtypeStruct(gram.shape,...]
    another operation x21 -> x0, matrix products: 31 us -> none  [the longest x11 16.6 us: inverses(): lax.linalg.triangular_solve(factor, identity, left_side=True, lower=True)]
    another operation x25 -> x0, local copies, waits for them, and re-layouts: 19.3 us -> none
    dot_general x3 -> x1, matrix products: 17.9 us -> 6.26 us  [mm(): lax.dot_general(a, b, (((1,), (0,)), ((), ())), precision=prec or PREC, p...]
    dot_general x2 -> x4, matrix products: 16.6 us -> 16.7 us  [contract_cols(): lax.dot_general(left, right, (((1,), (1,)), ((), ())), precision=lax.Prec...]
  transfers between devices with their start and end apart: 4 -> 4, of which waited for: 3 -> 3; matrix products, arithmetic and copies ran while one was open for 54% -> 0% of each run, Pallas kernels for 0% -> 16%
where the time goes in v1:
time: 232 us; the launch traced here: 231 us
  waiting for transfers between devices  156 us (67%)
  Pallas kernels  37.9 us (16%)
  matrix products  23 us (10%)
  between operations  13.8 us (6%)
    psum x1, waiting for transfers between devices, per_device(): gram_rows, crosst_rows = lax.psum((gram_part, crosst_part), 'atoms')  80.4 us
    all_gather x1, waiting for transfers between devices, per_device(): full_modes = lax.all_gather(subspace, 'modes', axis=0, tiled=True)  50.7 us
    pallas_call x1, Pallas kernels, cholesky_inverse(): pl.pallas_call(inverse_kernel, out_shape=jax.ShapeDtypeStruct(gram.shape,...  37.9 us
    all_gather x1, waiting for transfers between devices, per_device(): gram_full = lax.all_gather(gram_rows, 'modes', axis=0, tiled=True)  24.2 us
    dot_general x4, matrix products, contract_cols(): lax.dot_general(left, right, (((1,), (1,)), ((), ())), precision=lax.Prec...  16.7 us
    dot_general x1, matrix products, mm(): lax.dot_general(a, b, (((1,), (0,)), ((), ())), precision=prec or PREC, p...  6.26 us
  transfers between devices with their start and end apart: 4, of which 3 were waited for; matrix products, arithmetic and copies ran while one was open for 0% of the time, Pallas kernels for 16%

profile of v1, /device:TPU:0, one launch (start us, length us, event | category | flops | bytes accessed | tf_op | source)
XLA Modules:
  0.0 231.5 jit_solution(8858763305396009763)
XLA Ops:
  7.2 0.0 copy-start
  7.2 0.0 copy-start.2
  7.2 0.0 all-gather.4.cloned.1.call-start
  7.2 0.7 all-gather.4.cloned.1.call-update
  7.9 0.0 all-reduce.3.cloned.1.call-start
  8.0 50.7 %all-gather.4.cloned.1.call-done = f32[768,2048]{1,0:T(8,128)} async-done(((f32[192,2048]{1,0:T(8,128)}), f32[768,2048]{1,0:T(8,128)}) %all-gather.4.cloned.1.call-update) | async-done | bytes 6291472 | tf_op jit(solution)/shard_map/all_gather | solution.py:109
  58.7 0.0 copy-done.2
  58.7 0.0 copy-start.1
  58.7 7.1 %convolution_multiply_fusion.1 = f32[192,768]{1,0:T(8,128)} fusion(f32[192,2048]{1,0:T(8,128)S(1)} %copy-done.2, f32[768,2048]{1,0:T(8,128)} %all-gather.4.cloned.1.call-done), kind=kOutput, calls=%fused_computation.1 | convolution fusion | flops 1812086784 | bytes 8454144 | tf_op jit(solution)/shard_map/dot_general | solution.py:100
  65.7 0.0 copy-done
  65.7 0.0 copy-done.1
  65.7 4.1 %convolution_multiply_fusion = f32[192,768]{1,0:T(8,128)} fusion(f32[192,2048]{1,0:T(8,128)S(1)} %copy-done, f32[768,2048]{1,0:T(8,128)S(1)} %copy-done.1), kind=kOutput, calls=%fused_computation | convolution fusion | flops 1812086784 | bytes 8454144 | tf_op jit(solution)/shard_map/dot_general | solution.py:100
  69.9 0.0 all-reduce.3.cloned.1.call-update
  69.9 0.0 all-gather.6.cloned.1.call-start
  69.9 80.4 %all-reduce.3.cloned.1.call-done = (f32[192,768]{1,0:T(8,128)}, f32[192,768]{1,0:T(8,128)}) async-done(((f32[192,768]{1,0:T(8,128)}, f32[192,768]{1,0:T(8,128)}), (f32[192,768]{1,0:T(8,128)}, f32[192,768]{1,0:T(8,128)})) %all-reduce.3.cloned.1.call-update) | async-done | bytes 1179664 | tf_op jit(solution)/shard_map/psum | solution.py:112
  150.4 0.0 all-gather.6.cloned.1.call-update
  150.4 0.2 all-gather.8.cloned.1.call-start
  150.6 0.3 all-gather.8.cloned.1.call-update
  151.0 24.2 %all-gather.6.cloned.1.call-done.g_ref = f32[768,768]{1,0:T(8,128)} async-done(((f32[192,768]{1,0:T(8,128)}), f32[768,768]{1,0:T(8,128)}) %all-gather.6.cloned.1.call-update) | async-done | bytes 2359312 | tf_op jit(solution)/shard_map/all_gather | solution.py:113
  175.2 37.9 %shard_map.41 = f32[768,768]{1,0:T(8,128)} custom-call(f32[768,768]{1,0:T(8,128)} %all-gather.6.cloned.1.call-done.g_ref), custom_call_target="tpu_custom_call" | custom-call | flops 49999998976 | bytes 4000000 | tf_op jit(solution)/shard_map/pallas_call | solution.py:90
  213.1 3.3 %fusion = f32[192,768]{1,0:T(8,128)S(1)} fusion(f32[768,768]{1,0:T(8,128)} %all-gather.8.cloned.1.call-done, f32[768,768]{1,0:T(8,128)} %shard_map.41, s32[]{:T(128)S(6)} %select_n.3), kind=kOutput, calls=%fused_computation.2 | convolution fusion | flops 679477248 | bytes 3538948 | tf_op jit(solution)/shard_map/dot_general | solution.py:100
  216.5 0.0 copy-done.3
  216.5 2.2 fusion.6
  218.7 6.3 %fusion.2 = f32[192,2048]{1,0:T(8,128)} fusion(f32[768,2048]{1,0:T(8,128)} %all-gather.4.cloned.1.call-done, f32[768,768]{1,0:T(8,128)S(1)} %copy-done.3, s32[]{:T(128)S(6)} %select_n.3), kind=kOutput, calls=%fused_computation.4 | convolution fusion | flops 1811939328 | bytes 8454148 | tf_op jit(solution)/shard_map/dot_general | solution.py:14
  (2 shorter events, 0.0 us)
Async XLA Ops:
  7.2 58.6 %copy-start = (f32[192,2048]{1,0:T(8,128)S(1)}, f32[192,2048]{1,0:T(8,128)}, u32[]{:S(2)}) copy-start(f32[192,2048]{1,0:T(8,128)} %param.3) | copy-start | bytes 4718596
  7.2 51.5 %copy-start.2 = (f32[192,2048]{1,0:T(8,128)S(1)}, f32[192,2048]{1,0:T(8,128)}, u32[]{:S(2)}) copy-start(f32[192,2048]{1,0:T(8,128)} %param.2) | copy-start | bytes 4718596
  7.2 51.5 %all-gather.4.cloned.1.call-start = ((), (), s32[]{:S(2)}) async-start(), calls=%async_computation | async-start | bytes 7864320 | tf_op jit(solution)/shard_map/all_gather | solution.py:109
  7.9 142.4 %all-reduce.3.cloned.1.call-start = ((), (), s32[]{:S(2)}) async-start(), calls=%async_computation.3 | async-start | bytes 2359296 | tf_op jit(solution)/shard_map/psum | solution.py:112
  58.7 7.1 %copy-start.1 = (f32[768,2048]{1,0:T(8,128)S(1)}, f32[768,2048]{1,0:T(8,128)}, u32[]{:S(2)}) copy-start(f32[768,2048]{1,0:T(8,128)} %all-gather.4.cloned.1.call-done) | copy-start | bytes 18874372
  69.9 105.3 %all-gather.6.cloned.1.call-start = ((), (), s32[]{:S(2)}) async-start(), calls=%async_computation.1 | async-start | bytes 2949120 | tf_op jit(solution)/shard_map/all_gather | solution.py:113
  150.4 62.7 %all-gather.8.cloned.1.call-start = ((), (), s32[]{:S(2)}) async-start(), calls=%async_computation.2 | async-start | bytes 2949120 | tf_op jit(solution)/shard_map/all_gather | solution.py:114
  213.1 3.3 %copy-start.3 = (f32[768,768]{1,0:T(8,128)S(1)}, f32[768,768]{1,0:T(8,128)}, u32[]{:S(2)}) copy-start(f32[768,768]{1,0:T(8,128)} %shard_map.41) | copy-start | bytes 7077892
Sparse Core Ops, SparseCore 0:
  9.6 49.0 all-gather.3
  70.0 80.3 all-reduce.2
  151.9 23.2 all-gather.5
  176.6 24.0 all-gather.7

commit v2 on v1

--- a/solution.py
+++ b/solution.py
@@ -1,9 +1,15 @@
+import functools
+
 import jax
 import jax.numpy as jnp
 from jax import lax
 from jax.experimental import pallas as pl
 from jax.experimental.pallas import tpu as pltpu
 from jax.sharding import PartitionSpec as P
+
+HIGH = lax.Precision.HIGH
+VMEM = pl.BlockSpec(memory_space=pltpu.VMEM)
+ANY = pl.BlockSpec(memory_space=pl.ANY)
 
 LANES = 128
 SUB = 32
@@ -58,10 +64,158 @@
     return jnp.where(c <= r, full, 0.0)
 
 
-def inverse_kernel(g_ref, x_ref):
-    size = g_ref.shape[0]
-    n = size // LANES
-    x_ref[...] = g_ref[...]
+def nt(a, b, prec=HIGH):
+    return lax.dot_general(a, b, (((1,), (1,)), ((), ())), precision=prec, preferred_element_type=jnp.float32)
+
+
+def bits(axis):
+    return range(lax.axis_size(axis).bit_length() - 1)
+
+
+def swap(x, axis, bit):
+    return lax.ppermute(x, axis, [(i, i ^ (1 << bit)) for i in range(lax.axis_size(axis))])
+
+
+def side(axis, bit):
+    return (lax.axis_index(axis) >> bit) & 1
+
+
+def reduce_scatter_bit(x, axis, bit):
+    half = x.shape[0] // 2
+    b = side(axis, bit)
+    send = lax.dynamic_slice_in_dim(x, (1 - b) * half, half, 0)
+    return lax.dynamic_slice_in_dim(x, b * half, half, 0) + swap(send, axis, bit)
+
+
+def all_gather_bit(x, axis, bit):
+    other = swap(x, axis, bit)
+    first = side(axis, bit) == 0
+    return jnp.concatenate([jnp.where(first, x, other), jnp.where(first, other, x)], 0)
+
+
+def all_reduce_atoms(x):
+    order = list(bits("atoms"))
+    scattered = []
+    for b in order:
+        if b != order[-1] and x.shape[0] % 16 == 0:
+            x = reduce_scatter_bit(x, "atoms", b)
+            scattered.append(b)
+        else:
+            x = x + swap(x, "atoms", b)
+    for b in reversed(scattered):
+        x = all_gather_bit(x, "atoms", b)
+    return x
+
+
+def all_gather_modes(x):
+    shape = x.shape
+    x = x[None]
+    for b in reversed(bits("modes")):
+        other = swap(x, "modes", b)
+        first = side("modes", b) == 0
+        x = jnp.stack([jnp.where(first, x, other), jnp.where(first, other, x)], 1).reshape((-1,) + shape)
+    return x.reshape(-1, shape[1])
+
+
+def gather_pieces(x):
+    width = x.shape[1]
+    half = width // 2
+    out = []
+    for start in (0, half):
+        part = x[:, start : start + half]
+        held = [(0, part)]
+        for b in reversed(bits("modes")):
+            held += [(mask ^ (1 << b), swap(piece, "modes", b)) for mask, piece in held]
+        out += [(mask, start, piece) for mask, piece in held]
+    return out
+
+
+def load_pieces(meta, index_ref, refs, scratch, sem):
+    rows = refs[0].shape[0]
+    copies = []
+    for i, ((mask, start), ref) in enumerate(zip(meta, refs)):
+        row = pl.multiple_of((index_ref[0] ^ mask) * rows, 8)
+        copies.append(
+            pltpu.make_async_copy(ref, scratch.at[pl.ds(row, rows), pl.ds(start, ref.shape[1])], sem.at[i])
+        )
+    for copy in copies:
+        copy.start()
+    return copies
+
+
+def gram_kernel(meta, total, index_ref, blocks_ref, *refs):
+    pieces, (out_ref, scratch, sem) = refs[: len(meta)], refs[len(meta) :]
+    for copy in load_pieces(meta, index_ref, pieces, scratch, sem):
+        copy.wait()
+    count = out_ref.shape[0] // LANES
+    depth = scratch.shape[1]
+    chunk = min(512, depth)
+
+    def block(i, _):
+        p = pl.multiple_of(blocks_ref[0, i] * LANES, LANES)
+        t = pl.multiple_of(blocks_ref[1, i] * LANES, LANES)
+        acc = jnp.zeros((LANES, LANES), jnp.float32)
+        for k in range(0, depth, chunk):
+            acc += nt(scratch[pl.ds(p, LANES), k : k + chunk], scratch[pl.ds(t, LANES), k : k + chunk])
+        out_ref[pl.ds(pl.multiple_of(i * LANES, LANES), LANES), :] = acc / total
+        return 0
+
+    lax.fori_loop(0, count, block, 0)
+
+
+def cross_kernel(meta, total, index_ref, applied_ref, *refs):
+    pieces, (out_ref, scratch, sem) = refs[: len(meta)], refs[len(meta) :]
+    for copy in load_pieces(meta, index_ref, pieces, scratch, sem):
+        copy.wait()
+    depth = scratch.shape[1]
+    chunk = min(512, depth)
+    wide = 2 * LANES
+
+    def block(i, _):
+        at = pl.multiple_of(i * wide, wide)
+        acc = jnp.zeros((out_ref.shape[0], wide), jnp.float32)
+        for k in range(0, depth, chunk):
+            acc += nt(applied_ref[:, k : k + chunk], scratch[pl.ds(at, wide), k : k + chunk])
+        out_ref[:, pl.ds(at, wide)] = acc / total
+        return 0
+
+    lax.fori_loop(0, out_ref.shape[1] // wide, block, 0)
+
+
+def final_kernel(meta, index_ref, inv_ref, crosst_ref, *refs):
+    pieces, (ortho_ref, proj_ref, scratch, sem) = refs[: len(meta)], refs[len(meta) :]
+    copies = load_pieces(meta, index_ref, pieces, scratch, sem)
+    rows = ortho_ref.shape[0]
+    mine = pl.ds(pl.multiple_of(index_ref[0] * rows, 8), rows)
+    half = nt(inv_ref[mine, :], crosst_ref[...])
+    proj_ref[...] = nt(half, inv_ref[...])
+    for copy in copies:
+        copy.wait()
+    chunk = min(512, ortho_ref.shape[1])
+
+    def block(i, _):
+        at = pl.multiple_of(i * chunk, chunk)
+        ortho_ref[:, pl.ds(at, chunk)] = mm(inv_ref[mine, :], scratch[:, pl.ds(at, chunk)], HIGH)
+        return 0
+
+    lax.fori_loop(0, ortho_ref.shape[1] // chunk, block, 0)
+
+
+def cost(flops, moved):
+    return pl.CostEstimate(flops=int(flops), bytes_accessed=int(moved), transcendentals=0)
+
+
+def inverse_kernel(n, packed_ref, x_ref):
+    size = x_ref.shape[0]
+    i = 0
+    for p in range(n):
+        for t in range(n):
+            spot = (slice(LANES * p, LANES * (p + 1)), slice(LANES * t, LANES * (t + 1)))
+            if t >= p:
+                x_ref[spot] = packed_ref[LANES * i : LANES * (i + 1), :]
+                i += 1
+            else:
+                x_ref[spot] = jnp.zeros((LANES, LANES), jnp.float32)
 
     def at(t):
         return pl.ds(pl.multiple_of(t * LANES, LANES), LANES)
@@ -86,38 +240,68 @@
         x_ref[LANES * t : LANES * (t + 1), LANES * (t + 1) :] = jnp.zeros((LANES, size - LANES * (t + 1)), jnp.float32)
 
 
-def cholesky_inverse(gram):
+def per_device(subspace, applied):
+    width, depth = subspace.shape
+    size = width * lax.axis_size("modes")
+    total = depth * lax.axis_size("atoms")
+    panels = size // LANES
+    upper = [(p, t) for p in range(panels) for t in range(p, panels)]
+    per = -(-len(upper) // lax.axis_size("modes"))
+    table = jnp.array((upper + upper[-1:] * (per * lax.axis_size("modes") - len(upper))), jnp.int32).T
+    index = lax.axis_index("modes")
+    mine = lax.dynamic_slice_in_dim(table, index * per, per, 1)
+    index = index[None]
+
+    found = gather_pieces(subspace)
+    meta = tuple((mask, start) for mask, start, _ in found)
+    pieces = [piece for _, _, piece in found]
+    smem = pl.BlockSpec(memory_space=pltpu.SMEM)
+    scratch = [pltpu.VMEM((size, depth), jnp.float32), pltpu.SemaphoreType.DMA((len(pieces),))]
+
+    gram = pl.pallas_call(
+        functools.partial(gram_kernel, meta, float(total)),
+        out_shape=jax.ShapeDtypeStruct((per * LANES, LANES), jnp.float32),
+        in_specs=[smem, smem] + [ANY] * len(pieces),
+        out_specs=VMEM,
+        scratch_shapes=scratch,
+        cost_estimate=cost(2e9, 8e6),
+        name="gram",
+    )(index, mine, *pieces)
+    gram = all_reduce_atoms(gram)
+    gram = all_gather_modes(gram)
+
+    crosst = pl.pallas_call(
+        functools.partial(cross_kernel, meta, float(total)),
+        out_shape=jax.ShapeDtypeStruct((width, size), jnp.float32),
+        in_specs=[smem, VMEM] + [ANY] * len(pieces),
+        out_specs=VMEM,
+        scratch_shapes=scratch,
+        cost_estimate=cost(4e9, 8e6),
+        name="cross",
+    )(index, applied, *pieces)
+    crosst = all_reduce_atoms(crosst)
+    crosst = all_gather_modes(crosst)
+
+    inv_lower = pl.pallas_call(
+        functools.partial(inverse_kernel, panels),
+        out_shape=jax.ShapeDtypeStruct((size, size), jnp.float32),
+        in_specs=[VMEM],
+        out_specs=VMEM,
+        cost_estimate=cost(20e9, 4e6),
+        name="inverse",
+    )(gram)
     return pl.pallas_call(
-        inverse_kernel,
-        out_shape=jax.ShapeDtypeStruct(gram.shape, jnp.float32),
-        in_specs=[pl.BlockSpec(memory_space=pltpu.VMEM)],
-        out_specs=pl.BlockSpec(memory_space=pltpu.VMEM),
-        cost_estimate=pl.CostEstimate(flops=50_000_000_000, bytes_accessed=4_000_000, transcendentals=0),
-    )(gram)
-
-
-def contract_cols(left, right):
-    return lax.dot_general(
-        left, right, (((1,), (1,)), ((), ())), precision=lax.Precision.HIGH, preferred_element_type=jnp.float32
-    )
-
-
-def per_device(subspace, applied):
-    mode_width = subspace.shape[0]
-    row_total = subspace.shape[1] * lax.axis_size("atoms")
-    mode_start = lax.axis_index("modes") * mode_width
-    full_modes = lax.all_gather(subspace, "modes", axis=0, tiled=True)
-    gram_part = contract_cols(subspace, full_modes) / row_total
-    crosst_part = contract_cols(applied, full_modes) / row_total
-    gram_rows, crosst_rows = lax.psum((gram_part, crosst_part), "atoms")
-    gram_full = lax.all_gather(gram_rows, "modes", axis=0, tiled=True)
-    crosst_full = lax.all_gather(crosst_rows, "modes", axis=0, tiled=True)
-    inv_lower = cholesky_inverse(gram_full)
-    lower_rows = lax.dynamic_slice_in_dim(inv_lower, mode_start, mode_width, 0)
-    high = lax.Precision.HIGH
-    ortho_basis = mm(lower_rows, full_modes, high)
-    projected = contract_cols(contract_cols(lower_rows, crosst_full), inv_lower)
-    return (ortho_basis, projected)
+        functools.partial(final_kernel, meta),
+        out_shape=(
+            jax.ShapeDtypeStruct((width, depth), jnp.float32),
+            jax.ShapeDtypeStruct((width, size), jnp.float32),
+        ),
+        in_specs=[smem, VMEM, VMEM] + [ANY] * len(pieces),
+        out_specs=(VMEM, VMEM),
+        scratch_shapes=scratch,
+        cost_estimate=cost(4e9, 8e6),
+        name="final",
+    )(index, inv_lower, crosst, *pieces)
 
 
 def solution(mesh):

time: 232 us -> 168 us (0.72)
  waiting for transfers between devices: 156 us -> 71.7 us
  Pallas kernels: 37.9 us -> 63.2 us
  matrix products: 23 us -> 0 us
  starting transfers between devices: 0.34 us -> 20.4 us
  between operations: 13.8 us -> 0.86 us
  local copies, waits for them, and re-layouts: 0.02 us -> 7.1 us
  other arithmetic: 0 us -> 4.16 us
    psum x1 -> x0, waiting for transfers between devices: 80.4 us -> none  [per_device(): gram_rows, crosst_rows = lax.psum((gram_part, crosst_part), 'atoms')]
    all_gather x3 -> x0, waiting for transfers between devices: 74.9 us -> none  [the longest x1 50.7 us: per_device(): full_modes = lax.all_gather(subspace, 'modes', axis=0, tiled=True)]
    ppermute x0 -> x20, waiting for transfers between devices: none -> 71.7 us  [swap(): lax.ppermute(x, axis, [(i, i ^ 1 << bit) for i in range(lax.axis_size(axi...]
    pallas_call x1 -> x4, Pallas kernels: 37.9 us -> 63.2 us  [the longest x1 37.6 us: per_device(): pl.pallas_call(functools.partial(inverse_kernel, panels), out_shape=jax.S...]
    dot_general x5 -> x0, matrix products: 23 us -> none  [the longest x4 16.7 us: contract_cols(): lax.dot_general(left, right, (((1,), (1,)), ((), ())), precision=lax.Prec...]
    ppermute x0 -> x20, starting transfers between devices: none -> 20.4 us  [swap(): lax.ppermute(x, axis, [(i, i ^ 1 << bit) for i in range(lax.axis_size(axi...]
    another operation x0 -> x2, local copies, waits for them, and re-layouts: none -> 2.83 us  [all_gather_modes(): jnp.stack([jnp.where(first, x, other), jnp.where(first, other, x)], 1)]
    dynamic_slice x0 -> x5, local copies, waits for them, and re-layouts: none -> 2.76 us  [the longest x4 2.03 us: reduce_scatter_bit(): send = lax.dynamic_slice_in_dim(x, (1 - b) * half, half, 0)]
  transfers between devices with their start and end apart: 4 -> 20, of which waited for: 3 -> 13; matrix products, arithmetic and copies ran while one was open for 0% -> 4% of each run, Pallas kernels for 16% -> 28%
where the time goes in v2:
time: 168 us; the launch traced here: 167 us
  waiting for transfers between devices  71.7 us (43%)
  Pallas kernels  63.2 us (38%)
  starting transfers between devices  20.4 us (12%)
  local copies, waits for them, and re-layouts  7.1 us (4%)
  other arithmetic  4.16 us (2%)
    ppermute x20, waiting for transfers between devices, swap(): lax.ppermute(x, axis, [(i, i ^ 1 << bit) for i in range(lax.axis_size(axi...  71.7 us
    pallas_call x1, Pallas kernels, per_device(): pl.pallas_call(functools.partial(inverse_kernel, panels), out_shape=jax.S...  37.6 us
    ppermute x20, starting transfers between devices, swap(): lax.ppermute(x, axis, [(i, i ^ 1 << bit) for i in range(lax.axis_size(axi...  20.4 us
    pallas_call x1, Pallas kernels, per_device(): pl.pallas_call(functools.partial(final_kernel, meta), out_shape=(jax.Shap...  9.08 us
    pallas_call x1, Pallas kernels, per_device(): pl.pallas_call(functools.partial(cross_kernel, meta, float(total)), out_s...  8.66 us
    pallas_call x1, Pallas kernels, per_device(): pl.pallas_call(functools.partial(gram_kernel, meta, float(total)), out_sh...  7.87 us
  transfers between devices with their start and end apart: 20, of which 13 were waited for; matrix products, arithmetic and copies ran while one was open for 4% of the time, Pallas kernels for 28%

profile of v2, /device:TPU:0, one launch (start us, length us, event | category | flops | bytes accessed | tf_op | source)
XLA Modules:
  0.0 167.5 jit_solution(4790579283494782962)
XLA Ops:
  0.6 1.5 fusion.1
  2.1 3.1 %collective-permute-start = (f32[192,1024]{1,0:T(8,128)S(1)}, f32[192,1024]{1,0:T(8,128)S(1)}, u32[]{:S(2)}, u32[]{:S(2)}) collective-permute-start(f32[192,1024]{1,0:T(8,128)S(1)} %get-tuple-element.7.refs_0_), channel_id=1, source_target_pairs={{0,2},{1,3},{2,0},{3,1},{4,6},{5,7},{6,4},{7,5},{8,10},{9,11},{10,... | collective-permute-start | bytes 2359304 | tf_op jit(solution)/shard_map/ppermute | solution.py:76
  5.8 17.8 %collective-permute-done.refs_1_ = f32[192,1024]{1,0:T(8,128)S(1)} collective-permute-done((f32[192,1024]{1,0:T(8,128)S(1)}, f32[192,1024]{1,0:T(8,128)S(1)}, u32[]{:S(2)}, u32[]{:S(2)}) %collective-permute-start) | collective-permute-done | bytes 786464 | tf_op jit(solution)/shard_map/ppermute | solution.py:76
  23.6 16.0 %collective-permute-done.3.refs_5_ = f32[192,1024]{1,0:T(8,128)S(1)} collective-permute-done((f32[192,1024]{1,0:T(8,128)S(1)}, f32[192,1024]{1,0:T(8,128)S(1)}, u32[]{:S(2)}, u32[]{:S(2)}) %collective-permute-start.3) | collective-permute-done | bytes 786464 | tf_op jit(solution)/shard_map/ppermute | solution.py:76
  40.3 1.7 collective-permute-done.5.refs_7_
  42.0 7.9 %gram.1 = f32[768,128]{1,0:T(8,128)} custom-call(s32[1]{0:T(128)} %bitcast.index_ref, s32[2,6]{1,0:T(2,128)} %fusion.blocks_ref, f32[192,1024]{1,0:T(8,128)} %copy-done.1, f32[192,1024]{1,0:T(8,128)} %copy-done.5, f32[192,1024]{1,0:T(8,128)} %collective-permute-done.1.refs_2_, f32[192,1024]{1,0:T(8,128)} %collective-permute-done.2.refs_3_, ...), custom_call_target="tpu_custom_call" | custom-call | flops 2000000000 | bytes 8000000 | tf_op jit(solution)/shard_map/gram/pallas_call | solution.py:261
  50.9 1.8 %collective-permute-start.6 = (f32[384,128]{1,0:T(8,128)S(1)}, f32[384,128]{1,0:T(8,128)S(1)}, u32[]{:S(2)}, u32[]{:S(2)}) collective-permute-start(f32[384,128]{1,0:T(8,128)S(1)} %constant_dynamic-slice_fusion.3), channel_id=1, source_target_pairs={{0,4},{4,0},{8,12},{12,8},{16,20},{20,16},{24,28},{28,24},{1,5},{5... | collective-permute-start | bytes 589832 | tf_op jit(solution)/shard_map/ppermute | solution.py:76
  52.7 8.7 %cross.1 = f32[192,768]{1,0:T(8,128)} custom-call(s32[1]{0:T(128)} %bitcast.index_ref, f32[192,2048]{1,0:T(8,128)} %applied_ref.1, f32[192,1024]{1,0:T(8,128)} %copy-done.1, f32[192,1024]{1,0:T(8,128)} %copy-done.5, f32[192,1024]{1,0:T(8,128)} %collective-permute-done.1.refs_2_, f32[192,1024]{1,0:T(8,128)} %collective-permute-done.2.refs_3_, ...), custom_call_target="tpu_custom_call" | custom-call | flops 4000000000 | bytes 8000000 | tf_op jit(solution)/shard_map/cross/pallas_call | solution.py:273
  62.8 1.9 %collective-permute-start.7 = (f32[192,128]{1,0:T(8,128)S(1)}, f32[192,128]{1,0:T(8,128)S(1)}, u32[]{:S(2)}, u32[]{:S(2)}) collective-permute-start(f32[192,128]{1,0:T(8,128)S(1)} %constant_dynamic-slice_fusion.2), channel_id=1, source_target_pairs={{0,8},{4,12},{8,0},{12,4},{16,24},{20,28},{24,16},{28,20},{1,9},{5... | collective-permute-start | bytes 294920 | tf_op jit(solution)/shard_map/ppermute | solution.py:76
  64.7 6.5 %collective-permute-done.13 = f32[96,768]{1,0:T(8,128)S(1)} collective-permute-done((f32[96,768]{1,0:T(8,128)S(1)}, f32[96,768]{1,0:T(8,128)S(1)}, u32[]{:S(2)}, u32[]{:S(2)}) %collective-permute-start.13) | collective-permute-done | bytes 294944 | tf_op jit(solution)/shard_map/ppermute | solution.py:76
  71.3 1.6 collective-permute-start.14
  73.0 2.6 %collective-permute-start.8 = (f32[192,128]{1,0:T(8,128)S(1)}, f32[192,128]{1,0:T(8,128)S(1)}, u32[]{:S(2)}, u32[]{:S(2)}) collective-permute-start(f32[192,128]{1,0:T(8,128)S(1)} %dynamic-slice_add_fusion.3), channel_id=1, source_target_pairs={{0,16},{4,20},{8,24},{12,28},{16,0},{20,4},{24,8},{28,12},{1,17},{... | collective-permute-start | bytes 294920 | tf_op jit(solution)/shard_map/ppermute | solution.py:76
  75.6 2.0 %collective-permute-done.14 = f32[48,768]{1,0:T(8,128)S(1)} collective-permute-done((f32[48,768]{1,0:T(8,128)S(1)}, f32[48,768]{1,0:T(8,128)S(1)}, u32[]{:S(2)}, u32[]{:S(2)}) %collective-permute-start.14) | collective-permute-done | bytes 147488 | tf_op jit(solution)/shard_map/ppermute | solution.py:76
  77.7 2.2 %collective-permute-start.15 = (f32[48,768]{1,0:T(8,128)S(1)}, f32[48,768]{1,0:T(8,128)S(1)}, u32[]{:S(2)}, u32[]{:S(2)}) collective-permute-start(f32[48,768]{1,0:T(8,128)S(1)} %dynamic-slice_add_fusion.2), channel_id=1, source_target_pairs={{0,16},{4,20},{8,24},{12,28},{16,0},{20,4},{24,8},{28,12},{1,17},{... | collective-permute-start | bytes 442376 | tf_op jit(solution)/shard_map/ppermute | solution.py:76
  80.4 1.6 collective-permute-start.9
  82.1 4.3 %collective-permute-done.15 = f32[48,768]{1,0:T(8,128)S(1)} collective-permute-done((f32[48,768]{1,0:T(8,128)S(1)}, f32[48,768]{1,0:T(8,128)S(1)}, u32[]{:S(2)}, u32[]{:S(2)}) %collective-permute-start.15) | collective-permute-done | bytes 147488 | tf_op jit(solution)/shard_map/ppermute | solution.py:76
  87.3 4.3 %collective-permute-done.16 = f32[48,768]{1,0:T(8,128)S(1)} collective-permute-done((f32[48,768]{1,0:T(8,128)S(1)}, f32[48,768]{1,0:T(8,128)S(1)}, u32[]{:S(2)}, u32[]{:S(2)}) %collective-permute-start.16) | collective-permute-done | bytes 147488 | tf_op jit(solution)/shard_map/ppermute | solution.py:76
  94.5 4.6 %collective-permute-done.17 = f32[96,768]{1,0:T(8,128)S(1)} collective-permute-done((f32[96,768]{1,0:T(8,128)S(1)}, f32[96,768]{1,0:T(8,128)S(1)}, u32[]{:S(2)}, u32[]{:S(2)}) %collective-permute-start.17) | collective-permute-done | bytes 294944 | tf_op jit(solution)/shard_map/ppermute | solution.py:76
  99.2 1.7 %collective-permute-start.18 = (f32[1,192,768]{2,1,0:T(8,128)S(1)}, f32[1,192,768]{2,1,0:T(8,128)S(1)}, u32[]{:S(2)}, u32[]{:S(2)}) collective-permute-start(f32[1,192,768]{2,1,0:T(8,128)S(1)} %maximum_bitcast_fusion.2), channel_id=1, source_target_pairs={{0,2},{1,3},{2,0},{3,1},{4,6},{5,7},{6,4},{7,5},{8,10},{9,11},{10,... | collective-permute-start | bytes 1769480 | tf_op jit(solution)/shard_map/ppermute | solution.py:76
  100.9 4.2 %collective-permute-done.11 = f32[1,768,128]{2,1,0:T(8,128)S(1)} collective-permute-done((f32[1,768,128]{2,1,0:T(8,128)S(1)}, f32[1,768,128]{2,1,0:T(8,128)S(1)}, u32[]{:S(2)}, u32[]{:S(2)}) %collective-permute-start.11) | collective-permute-done | bytes 393248 | tf_op jit(solution)/shard_map/ppermute | solution.py:76
  106.1 8.9 %collective-permute-done.18 = f32[1,192,768]{2,1,0:T(8,128)S(1)} collective-permute-done((f32[1,192,768]{2,1,0:T(8,128)S(1)}, f32[1,192,768]{2,1,0:T(8,128)S(1)}, u32[]{:S(2)}, u32[]{:S(2)}) %collective-permute-start.18) | collective-permute-done | bytes 589856 | tf_op jit(solution)/shard_map/ppermute | solution.py:76
  118.8 37.6 %inverse.1.inv_ref = f32[768,768]{1,0:T(8,128)} custom-call(f32[3072,128]{1,0:T(8,128)} %bitcast.46), custom_call_target="tpu_custom_call" | custom-call | flops 20000000000 | bytes 4000000 | tf_op jit(solution)/shard_map/inverse/pallas_call | solution.py:285
  156.8 1.6 copy.6
  158.4 9.1 %final.1 = (f32[192,2048]{1,0:T(8,128)}, f32[192,768]{1,0:T(8,128)}) custom-call(s32[1]{0:T(128)} %bitcast.index_ref, f32[768,768]{1,0:T(8,128)} %inverse.1.inv_ref, f32[768,768]{1,0:T(8,128)} %bitcast.45, f32[192,1024]{1,0:T(8,128)} %copy-done.1, f32[192,1024]{1,0:T(8,128)} %copy-done.5, f32[192,1024]{1,0:T(8,128)} %collective-permute-done.1.refs_2_, ...), custom_call_target="tpu_custom_call" | custom-call | flops 4000000000 | bytes 8000000 | tf_op jit(solution)/shard_map/final/pallas_call | solution.py:293
  (64 shorter events, 13.4 us)
Async XLA Ops:
  0.6 39.0 %copy-start.4 = (s32[24,2]{0,1:T(2,128)S(1)}, s32[24,2]{0,1:T(2,128)}, u32[]{:S(2)}) copy-start(s32[24,2]{0,1:T(2,128)} %constant.29.clone) | copy-start | bytes 580
  2.1 39.9 %copy-start = (f32[192,1024]{1,0:T(8,128)}, f32[192,1024]{1,0:T(8,128)S(1)}, u32[]{:S(2)}) copy-start(f32[192,1024]{1,0:T(8,128)S(1)} %get-tuple-element.6.refs_4_) | copy-start | bytes 2359300
  2.1 39.9 %copy-start.1 = (f32[192,1024]{1,0:T(8,128)}, f32[192,1024]{1,0:T(8,128)S(1)}, u32[]{:S(2)}) copy-start(f32[192,1024]{1,0:T(8,128)S(1)} %get-tuple-element.7.refs_0_) | copy-start | bytes 2359300
  2.1 21.5 %collective-permute-start = (f32[192,1024]{1,0:T(8,128)S(1)}, f32[192,1024]{1,0:T(8,128)S(1)}, u32[]{:S(2)}, u32[]{:S(2)}) collective-permute-start(f32[192,1024]{1,0:T(8,128)S(1)} %get-tuple-element.7.refs_0_), channel_id=1, source_target_pairs={{0,2},{1,3},{2,0},{3,1},{4,6},{5,7},{6,4},{7,5},{8,10},{9,11},{10,... | collective-permute-start | bytes 2359304 | tf_op jit(solution)/shard_map/ppermute | solution.py:76
  5.2 34.4 %collective-permute-start.3 = (f32[192,1024]{1,0:T(8,128)S(1)}, f32[192,1024]{1,0:T(8,128)S(1)}, u32[]{:S(2)}, u32[]{:S(2)}) collective-permute-start(f32[192,1024]{1,0:T(8,128)S(1)} %get-tuple-element.6.refs_4_), channel_id=1, source_target_pairs={{0,2},{1,3},{2,0},{3,1},{4,6},{5,7},{6,4},{7,5},{8,10},{9,11},{10,... | collective-permute-start | bytes 2359304 | tf_op jit(solution)/shard_map/ppermute | solution.py:76
  5.3 35.1 %collective-permute-start.1 = (f32[192,1024]{1,0:T(8,128)S(1)}, f32[192,1024]{1,0:T(8,128)}, u32[]{:S(2)}, u32[]{:S(2)}) collective-permute-start(f32[192,1024]{1,0:T(8,128)S(1)} %get-tuple-element.7.refs_0_), channel_id=1, source_target_pairs={{0,1},{1,0},{2,3},{3,2},{4,5},{5,4},{6,7},{7,6},{8,9},{9,8},{10,11... | collective-permute-start | bytes 2359304 | tf_op jit(solution)/shard_map/ppermute | solution.py:76
  5.3 35.1 %collective-permute-start.4 = (f32[192,1024]{1,0:T(8,128)S(1)}, f32[192,1024]{1,0:T(8,128)}, u32[]{:S(2)}, u32[]{:S(2)}) collective-permute-start(f32[192,1024]{1,0:T(8,128)S(1)} %get-tuple-element.6.refs_4_), channel_id=1, source_target_pairs={{0,1},{1,0},{2,3},{3,2},{4,5},{5,4},{6,7},{7,6},{8,9},{9,8},{10,11... | collective-permute-start | bytes 2359304 | tf_op jit(solution)/shard_map/ppermute | solution.py:76
  23.6 18.4 %copy-start.5 = (f32[192,1024]{1,0:T(8,128)}, f32[192,1024]{1,0:T(8,128)S(1)}, u32[]{:S(2)}) copy-start(f32[192,1024]{1,0:T(8,128)S(1)} %collective-permute-done.refs_1_) | copy-start | bytes 2359300
  23.6 16.7 %collective-permute-start.2 = (f32[192,1024]{1,0:T(8,128)S(1)}, f32[192,1024]{1,0:T(8,128)}, u32[]{:S(2)}, u32[]{:S(2)}) collective-permute-start(f32[192,1024]{1,0:T(8,128)S(1)} %collective-permute-done.refs_1_), channel_id=1, source_target_pairs={{0,1},{1,0},{2,3},{3,2},{4,5},{5,4},{6,7},{7,6},{8,9},{9,8},{10,11... | collective-permute-start | bytes 2359304 | tf_op jit(solution)/shard_map/ppermute | solution.py:76
  39.6 2.4 %collective-permute-start.5 = (f32[192,1024]{1,0:T(8,128)S(1)}, f32[192,1024]{1,0:T(8,128)}, u32[]{:S(2)}, u32[]{:S(2)}) collective-permute-start(f32[192,1024]{1,0:T(8,128)S(1)} %collective-permute-done.3.refs_5_), channel_id=1, source_target_pairs={{0,1},{1,0},{2,3},{3,2},{4,5},{5,4},{6,7},{7,6},{8,9},{9,8},{10,11... | collective-permute-start | bytes 2359304 | tf_op jit(solution)/shard_map/ppermute | solution.py:76
  50.9 11.9 %collective-permute-start.6 = (f32[384,128]{1,0:T(8,128)S(1)}, f32[384,128]{1,0:T(8,128)S(1)}, u32[]{:S(2)}, u32[]{:S(2)}) collective-permute-start(f32[384,128]{1,0:T(8,128)S(1)} %constant_dynamic-slice_fusion.3), channel_id=1, source_target_pairs={{0,4},{4,0},{8,12},{12,8},{16,20},{20,16},{24,28},{28,24},{1,5},{5... | collective-permute-start | bytes 589832 | tf_op jit(solution)/shard_map/ppermute | solution.py:76
  62.4 8.8 %collective-permute-start.13 = (f32[96,768]{1,0:T(8,128)S(1)}, f32[96,768]{1,0:T(8,128)S(1)}, u32[]{:S(2)}, u32[]{:S(2)}) collective-permute-start(f32[96,768]{1,0:T(8,128)S(1)} %constant_dynamic-slice_fusion.1), channel_id=1, source_target_pairs={{0,4},{4,0},{8,12},{12,8},{16,20},{20,16},{24,28},{28,24},{1,5},{5... | collective-permute-start | bytes 884744 | tf_op jit(solution)/shard_map/ppermute | solution.py:76
  62.8 10.1 %collective-permute-start.7 = (f32[192,128]{1,0:T(8,128)S(1)}, f32[192,128]{1,0:T(8,128)S(1)}, u32[]{:S(2)}, u32[]{:S(2)}) collective-permute-start(f32[192,128]{1,0:T(8,128)S(1)} %constant_dynamic-slice_fusion.2), channel_id=1, source_target_pairs={{0,8},{4,12},{8,0},{12,4},{16,24},{20,28},{24,16},{28,20},{1,9},{5... | collective-permute-start | bytes 294920 | tf_op jit(solution)/shard_map/ppermute | solution.py:76
  71.3 6.3 %collective-permute-start.14 = (f32[48,768]{1,0:T(8,128)S(1)}, f32[48,768]{1,0:T(8,128)S(1)}, u32[]{:S(2)}, u32[]{:S(2)}) collective-permute-start(f32[48,768]{1,0:T(8,128)S(1)} %constant_dynamic-slice_fusion), channel_id=1, source_target_pairs={{0,8},{4,12},{8,0},{12,4},{16,24},{20,28},{24,16},{28,20},{1,9},{5... | collective-permute-start | bytes 442376 | tf_op jit(solution)/shard_map/ppermute | solution.py:76
  73.0 7.5 %collective-permute-start.8 = (f32[192,128]{1,0:T(8,128)S(1)}, f32[192,128]{1,0:T(8,128)S(1)}, u32[]{:S(2)}, u32[]{:S(2)}) collective-permute-start(f32[192,128]{1,0:T(8,128)S(1)} %dynamic-slice_add_fusion.3), channel_id=1, source_target_pairs={{0,16},{4,20},{8,24},{12,28},{16,0},{20,4},{24,8},{28,12},{1,17},{... | collective-permute-start | bytes 294920 | tf_op jit(solution)/shard_map/ppermute | solution.py:76
  77.7 8.7 %collective-permute-start.15 = (f32[48,768]{1,0:T(8,128)S(1)}, f32[48,768]{1,0:T(8,128)S(1)}, u32[]{:S(2)}, u32[]{:S(2)}) collective-permute-start(f32[48,768]{1,0:T(8,128)S(1)} %dynamic-slice_add_fusion.2), channel_id=1, source_target_pairs={{0,16},{4,20},{8,24},{12,28},{16,0},{20,4},{24,8},{28,12},{1,17},{... | collective-permute-start | bytes 442376 | tf_op jit(solution)/shard_map/ppermute | solution.py:76
  80.4 6.1 %collective-permute-start.9 = (f32[192,128]{1,0:T(8,128)S(1)}, f32[192,128]{1,0:T(8,128)S(1)}, u32[]{:S(2)}, u32[]{:S(2)}) collective-permute-start(f32[192,128]{1,0:T(8,128)S(1)} %add.52), channel_id=1, source_target_pairs={{0,8},{4,12},{8,0},{12,4},{16,24},{20,28},{24,16},{28,20},{1,9},{5... | collective-permute-start | bytes 294920 | tf_op jit(solution)/shard_map/ppermute | solution.py:76
  86.4 5.2 %collective-permute-start.16 = (f32[48,768]{1,0:T(8,128)S(1)}, f32[48,768]{1,0:T(8,128)S(1)}, u32[]{:S(2)}, u32[]{:S(2)}) collective-permute-start(f32[48,768]{1,0:T(8,128)S(1)} %add.59), channel_id=1, source_target_pairs={{0,8},{4,12},{8,0},{12,4},{16,24},{20,28},{24,16},{28,20},{1,9},{5... | collective-permute-start | bytes 442376 | tf_op jit(solution)/shard_map/ppermute | solution.py:76
  86.6 6.4 %collective-permute-start.10 = (f32[384,128]{1,0:T(8,128)S(1)}, f32[384,128]{1,0:T(8,128)S(1)}, u32[]{:S(2)}, u32[]{:S(2)}) collective-permute-start(f32[384,128]{1,0:T(8,128)S(1)} %pad_maximum_fusion.3), channel_id=1, source_target_pairs={{0,4},{4,0},{8,12},{12,8},{16,20},{20,16},{24,28},{28,24},{1,5},{5... | collective-permute-start | bytes 589832 | tf_op jit(solution)/shard_map/ppermute | solution.py:76
  91.7 7.4 %collective-permute-start.17 = (f32[96,768]{1,0:T(8,128)S(1)}, f32[96,768]{1,0:T(8,128)S(1)}, u32[]{:S(2)}, u32[]{:S(2)}) collective-permute-start(f32[96,768]{1,0:T(8,128)S(1)} %pad_maximum_fusion.2), channel_id=1, source_target_pairs={{0,4},{4,0},{8,12},{12,8},{16,20},{20,16},{24,28},{28,24},{1,5},{5... | collective-permute-start | bytes 884744 | tf_op jit(solution)/shard_map/ppermute | solution.py:76
  93.1 12.1 %collective-permute-start.11 = (f32[1,768,128]{2,1,0:T(8,128)S(1)}, f32[1,768,128]{2,1,0:T(8,128)S(1)}, u32[]{:S(2)}, u32[]{:S(2)}) collective-permute-start(f32[1,768,128]{2,1,0:T(8,128)S(1)} %maximum_bitcast_fusion.3), channel_id=1, source_target_pairs={{0,2},{1,3},{2,0},{3,1},{4,6},{5,7},{6,4},{7,5},{8,10},{9,11},{10,... | collective-permute-start | bytes 1179656 | tf_op jit(solution)/shard_map/ppermute | solution.py:76
  99.2 15.8 %collective-permute-start.18 = (f32[1,192,768]{2,1,0:T(8,128)S(1)}, f32[1,192,768]{2,1,0:T(8,128)S(1)}, u32[]{:S(2)}, u32[]{:S(2)}) collective-permute-start(f32[1,192,768]{2,1,0:T(8,128)S(1)} %maximum_bitcast_fusion.2), channel_id=1, source_target_pairs={{0,2},{1,3},{2,0},{3,1},{4,6},{5,7},{6,4},{7,5},{8,10},{9,11},{10,... | collective-permute-start | bytes 1769480 | tf_op jit(solution)/shard_map/ppermute | solution.py:76
  106.1 10.1 %collective-permute-start.12 = (f32[2,768,128]{2,1,0:T(8,128)}, f32[2,768,128]{2,1,0:T(8,128)}, u32[]{:S(2)}, u32[]{:S(2)}) collective-permute-start(f32[2,768,128]{2,1,0:T(8,128)} %maximum_bitcast_fusion.1), channel_id=1, source_target_pairs={{0,1},{1,0},{2,3},{3,2},{4,5},{5,4},{6,7},{7,6},{8,9},{9,8},{10,11... | collective-permute-start | bytes 2359304 | tf_op jit(solution)/shard_map/ppermute | solution.py:76
  116.2 40.2 %collective-permute-start.19 = (f32[2,192,768]{2,1,0:T(8,128)}, f32[2,192,768]{2,1,0:T(8,128)S(1)}, u32[]{:S(2)}, u32[]{:S(2)}) collective-permute-start(f32[2,192,768]{2,1,0:T(8,128)} %maximum_bitcast_fusion), channel_id=1, source_target_pairs={{0,1},{1,0},{2,3},{3,2},{4,5},{5,4},{6,7},{7,6},{8,9},{9,8},{10,11... | collective-permute-start | bytes 3538952 | tf_op jit(solution)/shard_map/ppermute | solution.py:76
  (3 other events, 24.3 us)

commit v3 on v1

v3 whole, which is shorter than its diff:
```python
import functools

import jax
import jax.numpy as jnp
from jax import lax
from jax.experimental import pallas as pl
from jax.experimental.pallas import tpu as pltpu
from jax.sharding import PartitionSpec as P


HIGH = lax.Precision.HIGH
VMEM = pl.BlockSpec(memory_space=pltpu.VMEM)
ANY = pl.BlockSpec(memory_space=pl.ANY)

LANES = 128
SUB = 32
PREC = lax.Precision.HIGHEST


def mm(a, b, prec=None):
    return lax.dot_general(a, b, (((1,), (0,)), ((), ())), precision=prec or PREC, preferred_element_type=jnp.float32)


def base_factor(w, s):
    lane = lax.broadcasted_iota(jnp.int32, (SUB, LANES), 1)
    row = lax.broadcasted_iota(jnp.int32, (SUB, LANES), 0)
    sub = lax.broadcasted_iota(jnp.int32, (8, LANES), 0)

    def column(rows, k):
        return [jnp.broadcast_to(r[:, SUB * s + k : SUB * s + k + 1], (8, LANES)) for r in rows]

    def one(tile, r):
        return jnp.broadcast_to(tile[r : r + 1], (8, LANES))

    groups = SUB // 8
    first = [w[8 * g : 8 * (g + 1)] for g in range(groups)]
    in_block = (lane >= SUB * s) & (lane < SUB * (s + 1))
    own = jnp.where(in_block, (lane - SUB * s == row).astype(jnp.float32), w)
    held = [own[8 * g : 8 * (g + 1)] for g in range(groups)]
    raw = list(first)
    ahead = SUB // 2
    cols = {m: column(first[m // 8 :], m) for m in range(ahead)}
    scales = [jnp.ones((8, LANES), jnp.float32) for _ in range(groups)]
    for k in range(SUB):
        g, r = divmod(k, 8)
        if k == 8:
            for m in range(ahead, SUB):
                cols[m] = column(raw[m // 8 :], m)
        mine = cols.pop(k)
        pivot = one(mine[0], r)
        scales[g] = jnp.where(sub == r, lax.rsqrt(pivot), scales[g])
        inv = 1.0 / pivot
        mult = [t * inv for t in mine]
        mult[0] = jnp.where(sub > r, mult[0], 0.0)
        for m, tiles in cols.items():
            across = one(mine[m // 8 - g], m % 8)
            cols[m] = [t - mult[i + m // 8 - g] * across for i, t in enumerate(tiles)]
        base = one(held[g], r)
        if k < 8:
            across = one(raw[g], r)
            for i in range(g, groups):
                raw[i] = raw[i] - mult[i - g] * across
        for i in range(g, groups):
            held[i] = held[i] - mult[i - g] * base
    return jnp.concatenate([h * c for h, c in zip(held, scales)], 0)


def diag_factor(a):
    n = LANES // SUB
    blocks = [a[SUB * t : SUB * (t + 1)] for t in range(n)]
    lane = lax.broadcasted_iota(jnp.int32, (SUB, LANES), 1)
    for s in range(n):
        blocks[s] = base_factor(blocks[s], s)
        if s + 1 < n:
            coef = jnp.transpose(blocks[s])[SUB * (s + 1) :]
            delta = mm(coef, blocks[s])
            keep = (lane < SUB * s) | (lane >= SUB * (s + 1))
            for t in range(s + 1, n):
                blocks[t] = jnp.where(keep, blocks[t], 0.0) - delta[SUB * (t - s - 1) : SUB * (t - s)]
    full = jnp.concatenate(blocks, 0)
    r = lax.broadcasted_iota(jnp.int32, (LANES, LANES), 0)
    c = lax.broadcasted_iota(jnp.int32, (LANES, LANES), 1)
    return jnp.where(c <= r, full, 0.0)


def nt(a, b, prec=HIGH):
    return lax.dot_general(a, b, (((1,), (1,)), ((), ())), precision=prec, preferred_element_type=jnp.float32)


def bits(axis):
    return range(lax.axis_size(axis).bit_length() - 1)


def swap(x, axis, bit):
    return lax.ppermute(x, axis, [(i, i ^ (1 << bit)) for i in range(lax.axis_size(axis))])


def side(axis, bit):
    return (lax.axis_index(axis) >> bit) & 1


def reduce_scatter_bit(x, axis, bit):
    half = x.shape[0] // 2
    b = side(axis, bit)
    send = lax.dynamic_slice_in_dim(x, (1 - b) * half, half, 0)
    got = swap(send, axis, bit)
    return lax.dynamic_slice_in_dim(x, b * half, half, 0) + got


def all_gather_bit(x, axis, bit):
    other = swap(x, axis, bit)
    first = side(axis, bit) == 0
    return jnp.concatenate([jnp.where(first, x, other), jnp.where(first, other, x)], 0)


def all_reduce_atoms(x):
    order = list(bits("atoms"))
    scattered = []
    for b in order:
        if b != order[-1] and x.shape[0] % 16 == 0:
            x = reduce_scatter_bit(x, "atoms", b)
            scattered.append(b)
        else:
            got = swap(x, "atoms", b)
            x = x + got
    for b in reversed(scattered):
        x = all_gather_bit(x, "atoms", b)
    return x


def gather_modes_pair(x):
    shape = x.shape
    x = x[None]
    for b in reversed(bits("modes")):
        other = swap(x, "modes", b)
        if b == 0:
            return x, other
        first = side("modes", b) == 0
        x = jnp.stack([jnp.where(first, x, other), jnp.where(first, other, x)], 1).reshape((-1,) + shape)


def pick(pair, core, mode, rows):
    mine, other = pair
    group, which = divmod(mode, 2)
    return jnp.where(core == which, mine[group, rows, :], other[group, rows, :])


def load_pieces(index_ref, keep, pieces, lo, scratch, sem):
    copies = []
    hi = lo + scratch.shape[1]
    for (mask, start), ref in pieces:
        rows = ref.shape[0]
        row = pl.multiple_of(((index_ref[0] ^ mask) & keep) * rows, 8)
        left, right = max(lo, start), min(hi, start + ref.shape[1])
        if left < right:
            source = ref.at[:, pl.ds(left - start, right - left)]
            target = scratch.at[pl.ds(row, rows), pl.ds(left - lo, right - left)]
            copies.append(pltpu.make_async_copy(source, target, sem.at[len(copies)]))
    for copy in copies:
        copy.start()
    return copies


def products_kernel(meta, keep, lo, total, with_sum, index_ref, blocks_ref, base_ref, applied_ref, *refs):
    sums, refs = (refs[:1], refs[1:]) if with_sum else ((), refs)
    pieces, (out_ref, scratch, sem) = refs[: len(meta)], refs[len(meta) :]
    for copy in load_pieces(index_ref, keep, list(zip(meta, pieces)), lo, scratch, sem):
        copy.wait()
    depth = scratch.shape[1]
    chunk = min(512, depth)
    width = applied_ref.shape[0]
    count = blocks_ref.shape[1]

    def store(at, acc):
        acc = acc / total
        out_ref[at, :] = acc + sums[0][at, :] if with_sum else acc

    def block(i, _):
        p = pl.multiple_of(blocks_ref[0, i] * LANES, LANES)
        t = pl.multiple_of(blocks_ref[1, i] * LANES, LANES)
        acc = jnp.zeros((LANES, LANES), jnp.float32)
        for k in range(0, depth, chunk):
            acc += nt(scratch[pl.ds(p, LANES), k : k + chunk], scratch[pl.ds(t, LANES), k : k + chunk])
        store(pl.ds(pl.multiple_of(i * LANES, LANES), LANES), acc)
        return 0

    lax.fori_loop(0, count, block, 0)

    def cross(i, _):
        at = pl.ds(pl.multiple_of((base_ref[0] + i) * LANES, LANES), LANES)
        acc = jnp.zeros((width, LANES), jnp.float32)
        for k in range(0, depth, chunk):
            acc += nt(applied_ref[:, lo + k : lo + k + chunk], scratch[at, k : k + chunk])
        store(pl.ds(pl.multiple_of(count * LANES + i * width, 8), width), acc)
        return 0

    lax.fori_loop(0, (out_ref.shape[0] - count * LANES) // width, cross, 0)


def project_kernel(index_ref, inv_ref, mine_ref, other_ref, proj_ref, crosst):
    rows = proj_ref.shape[0]
    panels = crosst.shape[1] // LANES
    core = index_ref[0] & 1
    for m in range(crosst.shape[0] // rows):
        for j in range(panels):
            block = pick((mine_ref, other_ref), core, m, slice(rows * j, rows * (j + 1)))
            crosst[rows * m : rows * (m + 1), LANES * j : LANES * (j + 1)] = block
    mine = pl.ds(pl.multiple_of(index_ref[0] * rows, 8), rows)
    half = nt(inv_ref[mine, :], crosst[...])
    proj_ref[...] = nt(half, inv_ref[...])


def invert(x_ref, start, stop):
    size = x_ref.shape[0]
    n = size // LANES

    def at(t):
        return pl.ds(pl.multiple_of(t * LANES, LANES), LANES)

    def step(p, _):
        x = diag_factor(x_ref[at(p), at(p)])
        panel = mm(x, x_ref[at(p), :], HIGH)
        x_ref[at(p), :] = panel
        x_ref[at(p), at(p)] = x

        def trailing(t, _):
            coef = jnp.transpose(x_ref[at(p), at(t)])
            x_ref[at(t), at(p)] = jnp.zeros((LANES, LANES), jnp.float32)
            x_ref[at(t), :] = x_ref[at(t), :] - mm(coef, x_ref[at(p), :], HIGH)
            return 0

        lax.fori_loop(p + 1, n, trailing, 0)
        return 0

    lax.fori_loop(start, stop, step, 0)
    for t in range(n - 1 if stop == n else 0):
        x_ref[LANES * t : LANES * (t + 1), LANES * (t + 1) :] = jnp.zeros((LANES, size - LANES * (t + 1)), jnp.float32)


def spot(p, t):
    return slice(LANES * p, LANES * (p + 1)), slice(LANES * t, LANES * (t + 1))


def unpack_upper(pair, core, part, per, n, x_ref):
    i = 0
    modes = 2 * pair[0].shape[0]
    for p in range(n):
        for t in range(n):
            if t >= p:
                m, r = divmod(i, per)
                x_ref[spot(p, t)] = pick(pair, core, part * modes // 2 + m, slice(LANES * r, LANES * (r + 1)))
                i += 1
            else:
                x_ref[spot(p, t)] = jnp.zeros((LANES, LANES), jnp.float32)


def first_inverse_kernel(n, per, index_ref, mine_ref, other_ref, x_ref):
    unpack_upper((mine_ref, other_ref), index_ref[0] & 1, 0, per, n, x_ref)
    invert(x_ref, 0, 1)


def rest_inverse_kernel(n, held_ref, x_ref):
    x_ref[...] = held_ref[...]
    invert(x_ref, 1, n)


def second_inverse_kernel(n, per_own, per_across, meta, keep, index_ref, first_ref, own_mine, own_other, late_mine, late_other, *refs):
    pieces, (x_ref, ortho_ref, scratch, corner, work, sem) = refs[: len(meta)], refs[len(meta) :]
    copies = load_pieces(index_ref, keep, list(zip(meta, pieces)), 0, scratch, sem)
    core = index_ref[0] & 1
    size = n * LANES
    for p in range(n):
        for t in range(n):
            m, r = divmod(p * n + t, per_across)
            corner[spot(p, t)] = pick((late_mine, late_other), core, m, slice(LANES * r, LANES * (r + 1)))
    unpack_upper((own_mine, own_other), core, 1, per_own, n, work)
    first = first_ref[...]
    upper = mm(first, corner[...], HIGH)
    lower = jnp.transpose(upper)
    work[...] = work[...] - mm(lower, upper, HIGH)
    for p in range(n):
        for t in range(p):
            work[spot(p, t)] = jnp.zeros((LANES, LANES), jnp.float32)
    corner[...] = mm(lower, first, HIGH)
    invert(work, 0, n)
    x_ref[:size, :size] = first
    x_ref[:size, size:] = jnp.zeros((size, size), jnp.float32)
    x_ref[size:, size:] = work[...]
    x_ref[size:, :size] = -mm(work[...], corner[...], HIGH)
    rows = ortho_ref.shape[0]
    mine = pl.ds(pl.multiple_of(index_ref[0] * rows, 8), rows)
    for copy in copies:
        copy.wait()
    chunk = min(512, ortho_ref.shape[1])

    def block(i, _):
        at = pl.ds(pl.multiple_of(i * chunk, chunk), chunk)
        ortho_ref[:, at] = mm(x_ref[mine, :], scratch[:, at], HIGH)
        return 0

    lax.fori_loop(0, ortho_ref.shape[1] // chunk, block, 0)


def cost(flops, moved):
    return pl.CostEstimate(flops=int(flops), bytes_accessed=int(moved), transcendentals=0)


def share(blocks, parts, index):
    per = -(-len(blocks) // parts)
    table = jnp.array(blocks + blocks[-1:] * (per * parts - len(blocks)), jnp.int32).T
    return per, lax.dynamic_slice_in_dim(table, index * per, per, 1)


def per_device(subspace, applied):
    width, depth = subspace.shape
    modes = lax.axis_size("modes")
    size = width * modes
    total = float(depth * lax.axis_size("atoms"))
    top = modes.bit_length() - 2
    lower_bits = list(reversed(range(top)))
    n = size // 2 // LANES
    mode = lax.axis_index("modes")
    index = mode[None]
    cut = depth // 2

    near = [(0, 0, subspace)]
    far = []
    for lo, hi in ((0, cut), (cut, depth)):
        far.append([(1 << top, lo, swap(subspace[:, lo:hi], "modes", top))])
    for b in lower_bits:
        near += [(mask ^ (1 << b), lo, swap(piece, "modes", b)) for mask, lo, piece in near]
    for held in far:
        for b in lower_bits:
            held += [(mask ^ (1 << b), lo, swap(piece, "modes", b)) for mask, lo, piece in held]

    smem = pl.BlockSpec(memory_space=pltpu.SMEM)

    half_keep = modes // 2 - 1
    leading = side("modes", top) == 0
    own = [(p, t) for p in range(n) for t in range(p, n)]
    per_own, own_share = share(own, modes // 2, mode & half_keep)
    across = [(p, n + t) for p in range(n) for t in range(n)]
    per_across, across_share = share(across, modes, mode)

    def products(blocks, base, rows, keep, lo, span, pieces, sums=None):
        meta = tuple((mask, start) for mask, start, _ in pieces)
        given = [index, blocks, base, applied] + ([] if sums is None else [sums])
        return pl.pallas_call(
            functools.partial(products_kernel, meta, keep, lo, total, sums is not None),
            out_shape=jax.ShapeDtypeStruct((blocks.shape[1] * LANES + n * width, LANES), jnp.float32),
            in_specs=[smem] * 3 + [VMEM] * (len(given) - 3) + [ANY] * len(pieces),
            out_specs=VMEM,
            scratch_shapes=[pltpu.VMEM((rows, span), jnp.float32), pltpu.SemaphoreType.DMA((len(pieces),))],
            cost_estimate=cost(3e9, 4 * rows * span),
        )(*given, *[piece for _, _, piece in pieces])

    early = products(own_share, jnp.zeros((1,), jnp.int32), size // 2, half_keep, 0, depth, near)
    early = all_reduce_atoms(early)
    gram_own = gather_modes_pair(early[: per_own * LANES])

    other_base = jnp.where(leading, n, 0)[None]
    late = None
    for held in far:
        lo, span = held[0][1], held[0][2].shape[1]
        late = products(across_share, other_base, size, modes - 1, lo, span, near + held, late)
    late = all_reduce_atoms(late)
    gram_across = gather_modes_pair(late[: per_across * LANES])
    cross_own, cross_across = early[per_own * LANES :], late[per_across * LANES :]
    crosst = jnp.concatenate(
        [jnp.where(leading, cross_own, cross_across), jnp.where(leading, cross_across, cross_own)], 0
    )
    crosst = gather_modes_pair(crosst)

    first_call = pl.pallas_call(
        functools.partial(first_inverse_kernel, n, per_own),
        out_shape=jax.ShapeDtypeStruct((size // 2, size // 2), jnp.float32),
        in_specs=[smem, VMEM, VMEM],
        out_specs=VMEM,
        cost_estimate=cost(5e9, 1e6),
        name="inverse_first",
    )
    first = first_call(index, *gram_own)
    rest_call = pl.pallas_call(
        functools.partial(rest_inverse_kernel, n),
        out_shape=jax.ShapeDtypeStruct((size // 2, size // 2), jnp.float32),
        in_specs=[VMEM],
        out_specs=VMEM,
        cost_estimate=cost(10e9, 1e6),
        name="inverse_rest",
    )
    first = rest_call(first)

    pieces = near + far[0] + far[1]
    meta = tuple((mask, start) for mask, start, _ in pieces)
    second_call = pl.pallas_call(
        functools.partial(second_inverse_kernel, n, per_own, per_across, meta, modes - 1),
        out_shape=(
            jax.ShapeDtypeStruct((size, size), jnp.float32),
            jax.ShapeDtypeStruct((width, depth), jnp.float32),
        ),
        in_specs=[smem] + [VMEM] * 5 + [ANY] * len(pieces),
        out_specs=(VMEM, VMEM),
        scratch_shapes=[
            pltpu.VMEM((size, depth), jnp.float32),
            pltpu.VMEM((size // 2, size // 2), jnp.float32),
            pltpu.VMEM((size // 2, size // 2), jnp.float32),
            pltpu.SemaphoreType.DMA((len(pieces),)),
        ],
        cost_estimate=cost(20e9, 8e6),
        name="inverse_second",
    )
    inv_lower, ortho = second_call(index, first, *gram_own, *gram_across, *[piece for _, _, piece in pieces])
    projected = pl.pallas_call(
        project_kernel,
        out_shape=jax.ShapeDtypeStruct((width, size), jnp.float32),
        in_specs=[smem, VMEM, VMEM, VMEM],
        out_specs=VMEM,
        scratch_shapes=[pltpu.VMEM((size, size), jnp.float32)],
        cost_estimate=cost(2e9, 5e6),
        name="project",
    )(index, inv_lower, *crosst)
    return ortho, projected


def solution(mesh):
    return jax.shard_map(
        per_device,
        mesh=mesh,
        in_specs=(P("modes", "atoms"), P("modes", "atoms")),
        out_specs=(P("modes", "atoms"), P("modes", None)),
        check_vma=False,
    )
```

time: 232 us -> 154 us (0.66)
  waiting for transfers between devices: 156 us -> 63 us
  matrix products: 23 us -> 0 us
  Pallas kernels: 37.9 us -> 60.4 us
  starting transfers between devices: 0.34 us -> 20.6 us
  between operations: 13.8 us -> 0.98 us
  local copies, waits for them, and re-layouts: 0.02 us -> 7.61 us
    psum x1 -> x0, waiting for transfers between devices: 80.4 us -> none  [per_device(): gram_rows, crosst_rows = lax.psum((gram_part, crosst_part), 'atoms')]
    all_gather x3 -> x0, waiting for transfers between devices: 74.9 us -> none  [the longest x1 50.7 us: per_device(): full_modes = lax.all_gather(subspace, 'modes', axis=0, tiled=True)]
    ppermute x0 -> x21, waiting for transfers between devices: none -> 63 us  [swap(): lax.ppermute(x, axis, [(i, i ^ 1 << bit) for i in range(lax.axis_size(axi...]
    dot_general x5 -> x0, matrix products: 23 us -> none  [the longest x4 16.7 us: contract_cols(): lax.dot_general(left, right, (((1,), (1,)), ((), ())), precision=lax.Prec...]
    pallas_call x1 -> x7, Pallas kernels: 37.9 us -> 60.4 us  [the longest x3 21.8 us: products(): pl.pallas_call(functools.partial(products_kernel, meta, keep, lo, total,...]
    ppermute x0 -> x21, starting transfers between devices: none -> 20.6 us  [swap(): lax.ppermute(x, axis, [(i, i ^ 1 << bit) for i in range(lax.axis_size(axi...]
    dynamic_slice x0 -> x6, local copies, waits for them, and re-layouts: none -> 3.39 us  [the longest x4 2.03 us: reduce_scatter_bit(): send = lax.dynamic_slice_in_dim(x, (1 - b) * half, half, 0)]
    unnamed x8 -> x22, local copies, waits for them, and re-layouts: 0.02 us -> 2.72 us
  transfers between devices with their start and end apart: 4 -> 21, of which waited for: 3 -> 12; matrix products, arithmetic and copies ran while one was open for 0% -> 4% of each run, Pallas kernels for 16% -> 36%
where the time goes in v3:
time: 154 us; the launch traced here: 153 us
  waiting for transfers between devices  63 us (41%)
  Pallas kernels  60.4 us (39%)
  starting transfers between devices  20.6 us (13%)
  local copies, waits for them, and re-layouts  7.61 us (5%)
    ppermute x21, waiting for transfers between devices, swap(): lax.ppermute(x, axis, [(i, i ^ 1 << bit) for i in range(lax.axis_size(axi...  63 us
    pallas_call x3, Pallas kernels, products(): pl.pallas_call(functools.partial(products_kernel, meta, keep, lo, total,...  21.8 us
    ppermute x21, starting transfers between devices, swap(): lax.ppermute(x, axis, [(i, i ^ 1 << bit) for i in range(lax.axis_size(axi...  20.6 us
    pallas_call x1, Pallas kernels, per_device(): second_call(index, first, *gram_own, *gram_across, *[piece for _, _, piec...  18.8 us
    pallas_call x1, Pallas kernels, per_device(): first = rest_call(first)  8.55 us
    pallas_call x1, Pallas kernels, per_device(): first = first_call(index, *gram_own)  5.67 us
    pallas_call x1, Pallas kernels, per_device(): pl.pallas_call(project_kernel, out_shape=jax.ShapeDtypeStruct((width, siz...  5.59 us
  transfers between devices with their start and end apart: 21, of which 12 were waited for; matrix products, arithmetic and copies ran while one was open for 4% of the time, Pallas kernels for 36%

profile of v3, /device:TPU:0, one launch (start us, length us, event | category | flops | bytes accessed | tf_op | source)
XLA Modules:
  0.0 153.3 jit_solution(16502568556480011377)
XLA Ops:
  2.7 2.6 %collective-permute-start.8 = (f32[192,1024]{1,0:T(8,128)S(1)}, f32[192,1024]{1,0:T(8,128)S(1)}, u32[]{:S(2)}, u32[]{:S(2)}) collective-permute-start(f32[192,1024]{1,0:T(8,128)S(1)} %get-tuple-element.7), channel_id=1, source_target_pairs={{0,2},{1,3},{2,0},{3,1},{4,6},{5,7},{6,4},{7,5},{8,10},{9,11},{10,... | collective-permute-start | bytes 2359304 | tf_op jit(solution)/shard_map/ppermute | solution.py:95
  5.4 18.3 %collective-permute-done.8.refs_2_ = f32[192,1024]{1,0:T(8,128)S(1)} collective-permute-done((f32[192,1024]{1,0:T(8,128)S(1)}, f32[192,1024]{1,0:T(8,128)S(1)}, u32[]{:S(2)}, u32[]{:S(2)}) %collective-permute-start.8) | collective-permute-done | bytes 786464 | tf_op jit(solution)/shard_map/ppermute | solution.py:95
  24.4 16.0 %collective-permute-done.10.refs_3_.refs_4_ = f32[192,1024]{1,0:T(8,128)} collective-permute-done((f32[192,1024]{1,0:T(8,128)S(1)}, f32[192,1024]{1,0:T(8,128)}, u32[]{:S(2)}, u32[]{:S(2)}) %collective-permute-start.10) | collective-permute-done | bytes 786464 | tf_op jit(solution)/shard_map/ppermute | solution.py:95
  42.2 8.3 %shard_map.59 = f32[960,128]{1,0:T(8,128)} custom-call(s32[1]{0:T(128)} %bitcast.index_ref, s32[2,3]{1,0:T(2,128)} %fusion.blocks_ref, s32[1]{0:T(128)} %constant.12.clone.1.base_ref, f32[192,2048]{1,0:T(8,128)} %applied_ref.5, f32[192,2048]{1,0:T(8,128)} %refs_0_.5, f32[192,2048]{1,0:T(8,128)} %copy-done.7), custom_call_target="tpu_custom_call" | custom-call | flops 3000000000 | bytes 3145728 | tf_op jit(solution)/shard_map/pallas_call | solution.py:348
  51.5 1.8 %collective-permute-start.1 = (f32[480,128]{1,0:T(8,128)S(1)}, f32[480,128]{1,0:T(8,128)S(1)}, u32[]{:S(2)}, u32[]{:S(2)}) collective-permute-start(f32[480,128]{1,0:T(8,128)S(1)} %constant_dynamic-slice_fusion.4), channel_id=1, source_target_pairs={{0,4},{4,0},{8,12},{12,8},{16,20},{20,16},{24,28},{28,24},{1,5},{5... | collective-permute-start | bytes 737288 | tf_op jit(solution)/shard_map/ppermute | solution.py:95
  53.2 6.7 %shard_map.60.refs_0_ = f32[960,128]{1,0:T(8,128)} custom-call(s32[1]{0:T(128)} %bitcast.index_ref, s32[2,3]{1,0:T(2,128)} %fusion.1.blocks_ref, s32[1]{0:T(128)} %bitcast.7.base_ref, f32[192,2048]{1,0:T(8,128)} %applied_ref.5, f32[192,2048]{1,0:T(8,128)} %refs_0_.5, f32[192,2048]{1,0:T(8,128)} %copy-done.7, f32[192,1024]{1,0:T(8,128)} %copy-done.8, ...), custom_call_target="tpu_custom_call" | custom-call | flops 3000000000 | bytes 3145728 | tf_op jit(solution)/shard_map/pallas_call | solution.py:348
  60.0 6.9 %shard_map.61 = f32[960,128]{1,0:T(8,128)} custom-call(s32[1]{0:T(128)} %bitcast.index_ref, s32[2,3]{1,0:T(2,128)} %fusion.1.blocks_ref, s32[1]{0:T(128)} %bitcast.7.base_ref, f32[192,2048]{1,0:T(8,128)} %applied_ref.5, f32[960,128]{1,0:T(8,128)} %shard_map.60.refs_0_, f32[192,2048]{1,0:T(8,128)} %refs_0_.5, f32[192,2048]{1,0:T(8,128)} %copy-done.7, ...), custom_call_target="tpu_custom_call" | custom-call | flops 3000000000 | bytes 3145728 | tf_op jit(solution)/shard_map/pallas_call | solution.py:348
  68.3 1.9 %collective-permute-start.2 = (f32[240,128]{1,0:T(8,128)S(1)}, f32[240,128]{1,0:T(8,128)S(1)}, u32[]{:S(2)}, u32[]{:S(2)}) collective-permute-start(f32[240,128]{1,0:T(8,128)S(1)} %constant_dynamic-slice_fusion.3), channel_id=1, source_target_pairs={{0,8},{4,12},{8,0},{12,4},{16,24},{20,28},{24,16},{28,20},{1,9},{5... | collective-permute-start | bytes 368648 | tf_op jit(solution)/shard_map/ppermute | solution.py:95
  70.2 5.8 %collective-permute-done.12 = f32[480,128]{1,0:T(8,128)S(1)} collective-permute-done((f32[480,128]{1,0:T(8,128)S(1)}, f32[480,128]{1,0:T(8,128)S(1)}, u32[]{:S(2)}, u32[]{:S(2)}) %collective-permute-start.12) | collective-permute-done | bytes 245792 | tf_op jit(solution)/shard_map/ppermute | solution.py:95
  76.1 1.6 %collective-permute-start.13 = (f32[240,128]{1,0:T(8,128)S(1)}, f32[240,128]{1,0:T(8,128)S(1)}, u32[]{:S(2)}, u32[]{:S(2)}) collective-permute-start(f32[240,128]{1,0:T(8,128)S(1)} %constant_dynamic-slice_fusion), channel_id=1, source_target_pairs={{0,8},{4,12},{8,0},{12,4},{16,24},{20,28},{24,16},{28,20},{1,9},{5... | collective-permute-start | bytes 368648 | tf_op jit(solution)/shard_map/ppermute | solution.py:95
  77.8 2.6 %collective-permute-start.3 = (f32[240,128]{1,0:T(8,128)S(1)}, f32[240,128]{1,0:T(8,128)S(1)}, u32[]{:S(2)}, u32[]{:S(2)}) collective-permute-start(f32[240,128]{1,0:T(8,128)S(1)} %dynamic-slice_add_fusion.3), channel_id=1, source_target_pairs={{0,16},{4,20},{8,24},{12,28},{16,0},{20,4},{24,8},{28,12},{1,17},{... | collective-permute-start | bytes 368648 | tf_op jit(solution)/shard_map/ppermute | solution.py:95
  80.4 1.9 %collective-permute-done.13 = f32[240,128]{1,0:T(8,128)S(1)} collective-permute-done((f32[240,128]{1,0:T(8,128)S(1)}, f32[240,128]{1,0:T(8,128)S(1)}, u32[]{:S(2)}, u32[]{:S(2)}) %collective-permute-start.13) | collective-permute-done | bytes 122912 | tf_op jit(solution)/shard_map/ppermute | solution.py:95
  82.3 2.4 %collective-permute-start.14 = (f32[240,128]{1,0:T(8,128)S(1)}, f32[240,128]{1,0:T(8,128)S(1)}, u32[]{:S(2)}, u32[]{:S(2)}) collective-permute-start(f32[240,128]{1,0:T(8,128)S(1)} %dynamic-slice_add_fusion.2), channel_id=1, source_target_pairs={{0,16},{4,20},{8,24},{12,28},{16,0},{20,4},{24,8},{28,12},{1,17},{... | collective-permute-start | bytes 368648 | tf_op jit(solution)/shard_map/ppermute | solution.py:95
  84.8 4.1 %collective-permute-done.3 = f32[240,128]{1,0:T(8,128)S(1)} collective-permute-done((f32[240,128]{1,0:T(8,128)S(1)}, f32[240,128]{1,0:T(8,128)S(1)}, u32[]{:S(2)}, u32[]{:S(2)}) %collective-permute-start.3) | collective-permute-done | bytes 122912 | tf_op jit(solution)/shard_map/ppermute | solution.py:95
  88.9 2.1 %collective-permute-done.14 = f32[240,128]{1,0:T(8,128)S(1)} collective-permute-done((f32[240,128]{1,0:T(8,128)S(1)}, f32[240,128]{1,0:T(8,128)S(1)}, u32[]{:S(2)}, u32[]{:S(2)}) %collective-permute-start.14) | collective-permute-done | bytes 122912 | tf_op jit(solution)/shard_map/ppermute | solution.py:95
  91.1 3.8 %collective-permute-done.4 = f32[240,128]{1,0:T(8,128)S(1)} collective-permute-done((f32[240,128]{1,0:T(8,128)S(1)}, f32[240,128]{1,0:T(8,128)S(1)}, u32[]{:S(2)}, u32[]{:S(2)}) %collective-permute-start.4) | collective-permute-done | bytes 122912 | tf_op jit(solution)/shard_map/ppermute | solution.py:95
  97.2 6.3 %collective-permute-done.5 = f32[480,128]{1,0:T(8,128)S(1)} collective-permute-done((f32[480,128]{1,0:T(8,128)S(1)}, f32[480,128]{1,0:T(8,128)S(1)}, u32[]{:S(2)}, u32[]{:S(2)}) %collective-permute-start.5) | collective-permute-done | bytes 245792 | tf_op jit(solution)/shard_map/ppermute | solution.py:95
  103.5 1.6 %collective-permute-start.6 = (f32[1,384,128]{2,1,0:T(8,128)S(1)}, f32[1,384,128]{2,1,0:T(8,128)S(1)}, u32[]{:S(2)}, u32[]{:S(2)}) collective-permute-start(f32[1,384,128]{2,1,0:T(8,128)S(1)} %slice_bitcast_fusion.1), channel_id=1, source_target_pairs={{0,2},{1,3},{2,0},{3,1},{4,6},{5,7},{6,4},{7,5},{8,10},{9,11},{10,... | collective-permute-start | bytes 589832 | tf_op jit(solution)/shard_map/ppermute | solution.py:95
  107.8 2.3 %collective-permute-done.6 = f32[1,384,128]{2,1,0:T(8,128)S(1)} collective-permute-done((f32[1,384,128]{2,1,0:T(8,128)S(1)}, f32[1,384,128]{2,1,0:T(8,128)S(1)}, u32[]{:S(2)}, u32[]{:S(2)}) %collective-permute-start.6) | collective-permute-done | bytes 196640 | tf_op jit(solution)/shard_map/ppermute | solution.py:95
  110.3 1.7 %collective-permute-start.19 = (f32[1,1152,128]{2,1,0:T(8,128)S(1)}, f32[1,1152,128]{2,1,0:T(8,128)S(1)}, u32[]{:S(2)}, u32[]{:S(2)}) collective-permute-start(f32[1,1152,128]{2,1,0:T(8,128)S(1)} %maximum_bitcast_fusion.1), channel_id=1, source_target_pairs={{0,2},{1,3},{2,0},{3,1},{4,6},{5,7},{6,4},{7,5},{8,10},{9,11},{10,... | collective-permute-start | bytes 1769480 | tf_op jit(solution)/shard_map/ppermute | solution.py:95
  113.2 5.7 %inverse_first.1.held_ref = f32[384,384]{1,0:T(8,128)} custom-call(s32[1]{0:T(128)} %bitcast.index_ref, f32[2,384,128]{2,1,0:T(8,128)} %copy-done.3, f32[2,384,128]{2,1,0:T(8,128)} %copy-done.9), custom_call_target="tpu_custom_call" | custom-call | flops 5000000000 | bytes 1000000 | tf_op jit(solution)/shard_map/inverse_first/pallas_call | solution.py:382
  118.8 8.6 %inverse_rest.1.first_ref = f32[384,384]{1,0:T(8,128)} custom-call(f32[384,384]{1,0:T(8,128)} %inverse_first.1.held_ref), custom_call_target="tpu_custom_call" | custom-call | flops 10000000000 | bytes 1000000 | tf_op jit(solution)/shard_map/inverse_rest/pallas_call | solution.py:391
  128.8 18.8 %inverse_second.1 = (f32[768,768]{1,0:T(8,128)}, f32[192,2048]{1,0:T(8,128)}) custom-call(s32[1]{0:T(128)} %bitcast.index_ref, f32[384,384]{1,0:T(8,128)} %inverse_rest.1.first_ref, f32[2,384,128]{2,1,0:T(8,128)} %copy-done.3, f32[2,384,128]{2,1,0:T(8,128)} %copy-done.9, f32[2,384,128]{2,1,0:T(8,128)} %copy-done.4, f32[2,384,128]{2,1,0:T(8,128)} %copy-done.10, ...), custom_call_target="tpu_custom_call" | custom-call | flops 20000000000 | bytes 8000000 | tf_op jit(solution)/shard_map/inverse_second/pallas_call | solution.py:412
  147.7 5.6 %project.1 = f32[192,768]{1,0:T(8,128)} custom-call(s32[1]{0:T(128)} %bitcast.index_ref, f32[768,768]{1,0:T(8,128)} %get-tuple-element.5.inv_ref, f32[2,1152,128]{2,1,0:T(8,128)} %copy-done, f32[2,1152,128]{2,1,0:T(8,128)} %collective-permute-done.20.other_ref), custom_call_target="tpu_custom_call" | custom-call | flops 2000000000 | bytes 5000000 | tf_op jit(solution)/shard_map/project/pallas_call | solution.py:413
  (76 shorter events, 15.1 us)
Async XLA Ops:
  0.6 23.0 %copy-start.6 = (s32[6,2]{0,1:T(2,128)S(1)}, s32[6,2]{0,1:T(2,128)}, u32[]{:S(2)}) copy-start(s32[6,2]{0,1:T(2,128)} %constant.31.clone) | copy-start | bytes 148
  0.6 39.8 %copy-start.5 = (s32[12,2]{0,1:T(2,128)S(1)}, s32[12,2]{0,1:T(2,128)}, u32[]{:S(2)}) copy-start(s32[12,2]{0,1:T(2,128)} %constant.32.clone) | copy-start | bytes 292
  0.7 40.4 %collective-permute-start = (f32[192,2048]{1,0:T(8,128)}, f32[192,2048]{1,0:T(8,128)S(1)}, u32[]{:S(2)}, u32[]{:S(2)}) collective-permute-start(f32[192,2048]{1,0:T(8,128)} %refs_0_.5), channel_id=1, source_target_pairs={{0,1},{1,0},{2,3},{3,2},{4,5},{5,4},{6,7},{7,6},{8,9},{9,8},{10,11... | collective-permute-start | bytes 4718600 | tf_op jit(solution)/shard_map/ppermute | solution.py:95
  2.7 21.0 %collective-permute-start.8 = (f32[192,1024]{1,0:T(8,128)S(1)}, f32[192,1024]{1,0:T(8,128)S(1)}, u32[]{:S(2)}, u32[]{:S(2)}) collective-permute-start(f32[192,1024]{1,0:T(8,128)S(1)} %get-tuple-element.7), channel_id=1, source_target_pairs={{0,2},{1,3},{2,0},{3,1},{4,6},{5,7},{6,4},{7,5},{8,10},{9,11},{10,... | collective-permute-start | bytes 2359304 | tf_op jit(solution)/shard_map/ppermute | solution.py:95
  5.3 35.2 %collective-permute-start.10 = (f32[192,1024]{1,0:T(8,128)S(1)}, f32[192,1024]{1,0:T(8,128)}, u32[]{:S(2)}, u32[]{:S(2)}) collective-permute-start(f32[192,1024]{1,0:T(8,128)S(1)} %get-tuple-element.6), channel_id=1, source_target_pairs={{0,2},{1,3},{2,0},{3,1},{4,6},{5,7},{6,4},{7,5},{8,10},{9,11},{10,... | collective-permute-start | bytes 2359304 | tf_op jit(solution)/shard_map/ppermute | solution.py:95
  23.7 26.8 %copy-start.8 = (f32[192,1024]{1,0:T(8,128)}, f32[192,1024]{1,0:T(8,128)S(1)}, u32[]{:S(2)}) copy-start(f32[192,1024]{1,0:T(8,128)S(1)} %collective-permute-done.8.refs_2_) | copy-start | bytes 2359300
  23.7 29.6 %collective-permute-start.9 = (f32[192,1024]{1,0:T(8,128)S(1)}, f32[192,1024]{1,0:T(8,128)}, u32[]{:S(2)}, u32[]{:S(2)}) collective-permute-start(f32[192,1024]{1,0:T(8,128)S(1)} %collective-permute-done.8.refs_2_), channel_id=1, source_target_pairs={{0,1},{1,0},{2,3},{3,2},{4,5},{5,4},{6,7},{7,6},{8,9},{9,8},{10,11... | collective-permute-start | bytes 2359304 | tf_op jit(solution)/shard_map/ppermute | solution.py:95
  40.4 19.5 %collective-permute-start.11 = (f32[192,1024]{1,0:T(8,128)}, f32[192,1024]{1,0:T(8,128)}, u32[]{:S(2)}, u32[]{:S(2)}) collective-permute-start(f32[192,1024]{1,0:T(8,128)} %collective-permute-done.10.refs_3_.refs_4_), channel_id=1, source_target_pairs={{0,1},{1,0},{2,3},{3,2},{4,5},{5,4},{6,7},{7,6},{8,9},{9,8},{10,11... | collective-permute-start | bytes 2359304 | tf_op jit(solution)/shard_map/ppermute | solution.py:95
  51.5 16.8 %collective-permute-start.1 = (f32[480,128]{1,0:T(8,128)S(1)}, f32[480,128]{1,0:T(8,128)S(1)}, u32[]{:S(2)}, u32[]{:S(2)}) collective-permute-start(f32[480,128]{1,0:T(8,128)S(1)} %constant_dynamic-slice_fusion.4), channel_id=1, source_target_pairs={{0,4},{4,0},{8,12},{12,8},{16,20},{20,16},{24,28},{28,24},{1,5},{5... | collective-permute-start | bytes 737288 | tf_op jit(solution)/shard_map/ppermute | solution.py:95
  67.9 8.2 %collective-permute-start.12 = (f32[480,128]{1,0:T(8,128)S(1)}, f32[480,128]{1,0:T(8,128)S(1)}, u32[]{:S(2)}, u32[]{:S(2)}) collective-permute-start(f32[480,128]{1,0:T(8,128)S(1)} %constant_dynamic-slice_fusion.1), channel_id=1, source_target_pairs={{0,4},{4,0},{8,12},{12,8},{16,20},{20,16},{24,28},{28,24},{1,5},{5... | collective-permute-start | bytes 737288 | tf_op jit(solution)/shard_map/ppermute | solution.py:95
  68.3 9.4 %collective-permute-start.2 = (f32[240,128]{1,0:T(8,128)S(1)}, f32[240,128]{1,0:T(8,128)S(1)}, u32[]{:S(2)}, u32[]{:S(2)}) collective-permute-start(f32[240,128]{1,0:T(8,128)S(1)} %constant_dynamic-slice_fusion.3), channel_id=1, source_target_pairs={{0,8},{4,12},{8,0},{12,4},{16,24},{20,28},{24,16},{28,20},{1,9},{5... | collective-permute-start | bytes 368648 | tf_op jit(solution)/shard_map/ppermute | solution.py:95
  76.1 6.2 %collective-permute-start.13 = (f32[240,128]{1,0:T(8,128)S(1)}, f32[240,128]{1,0:T(8,128)S(1)}, u32[]{:S(2)}, u32[]{:S(2)}) collective-permute-start(f32[240,128]{1,0:T(8,128)S(1)} %constant_dynamic-slice_fusion), channel_id=1, source_target_pairs={{0,8},{4,12},{8,0},{12,4},{16,24},{20,28},{24,16},{28,20},{1,9},{5... | collective-permute-start | bytes 368648 | tf_op jit(solution)/shard_map/ppermute | solution.py:95
  77.8 11.1 %collective-permute-start.3 = (f32[240,128]{1,0:T(8,128)S(1)}, f32[240,128]{1,0:T(8,128)S(1)}, u32[]{:S(2)}, u32[]{:S(2)}) collective-permute-start(f32[240,128]{1,0:T(8,128)S(1)} %dynamic-slice_add_fusion.3), channel_id=1, source_target_pairs={{0,16},{4,20},{8,24},{12,28},{16,0},{20,4},{24,8},{28,12},{1,17},{... | collective-permute-start | bytes 368648 | tf_op jit(solution)/shard_map/ppermute | solution.py:95
  82.3 8.7 %collective-permute-start.14 = (f32[240,128]{1,0:T(8,128)S(1)}, f32[240,128]{1,0:T(8,128)S(1)}, u32[]{:S(2)}, u32[]{:S(2)}) collective-permute-start(f32[240,128]{1,0:T(8,128)S(1)} %dynamic-slice_add_fusion.2), channel_id=1, source_target_pairs={{0,16},{4,20},{8,24},{12,28},{16,0},{20,4},{24,8},{28,12},{1,17},{... | collective-permute-start | bytes 368648 | tf_op jit(solution)/shard_map/ppermute | solution.py:95
  88.9 6.0 %collective-permute-start.4 = (f32[240,128]{1,0:T(8,128)S(1)}, f32[240,128]{1,0:T(8,128)S(1)}, u32[]{:S(2)}, u32[]{:S(2)}) collective-permute-start(f32[240,128]{1,0:T(8,128)S(1)} %add.47), channel_id=1, source_target_pairs={{0,8},{4,12},{8,0},{12,4},{16,24},{20,28},{24,16},{28,20},{1,9},{5... | collective-permute-start | bytes 368648 | tf_op jit(solution)/shard_map/ppermute | solution.py:95
  91.0 5.4 %collective-permute-start.15 = (f32[240,128]{1,0:T(8,128)S(1)}, f32[240,128]{1,0:T(8,128)S(1)}, u32[]{:S(2)}, u32[]{:S(2)}) collective-permute-start(f32[240,128]{1,0:T(8,128)S(1)} %add.51), channel_id=1, source_target_pairs={{0,8},{4,12},{8,0},{12,4},{16,24},{20,28},{24,16},{28,20},{1,9},{5... | collective-permute-start | bytes 368648 | tf_op jit(solution)/shard_map/ppermute | solution.py:95
  94.9 8.5 %collective-permute-start.5 = (f32[480,128]{1,0:T(8,128)S(1)}, f32[480,128]{1,0:T(8,128)S(1)}, u32[]{:S(2)}, u32[]{:S(2)}) collective-permute-start(f32[480,128]{1,0:T(8,128)S(1)} %pad_maximum_fusion.2), channel_id=1, source_target_pairs={{0,4},{4,0},{8,12},{12,8},{16,20},{20,16},{24,28},{28,24},{1,5},{5... | collective-permute-start | bytes 737288 | tf_op jit(solution)/shard_map/ppermute | solution.py:95
  96.5 9.6 %collective-permute-start.16 = (f32[480,128]{1,0:T(8,128)S(1)}, f32[480,128]{1,0:T(8,128)S(1)}, u32[]{:S(2)}, u32[]{:S(2)}) collective-permute-start(f32[480,128]{1,0:T(8,128)S(1)} %pad_maximum_fusion.3), channel_id=1, source_target_pairs={{0,4},{4,0},{8,12},{12,8},{16,20},{20,16},{24,28},{28,24},{1,5},{5... | collective-permute-start | bytes 737288 | tf_op jit(solution)/shard_map/ppermute | solution.py:95
  103.5 6.6 %collective-permute-start.6 = (f32[1,384,128]{2,1,0:T(8,128)S(1)}, f32[1,384,128]{2,1,0:T(8,128)S(1)}, u32[]{:S(2)}, u32[]{:S(2)}) collective-permute-start(f32[1,384,128]{2,1,0:T(8,128)S(1)} %slice_bitcast_fusion.1), channel_id=1, source_target_pairs={{0,2},{1,3},{2,0},{3,1},{4,6},{5,7},{6,4},{7,5},{8,10},{9,11},{10,... | collective-permute-start | bytes 589832 | tf_op jit(solution)/shard_map/ppermute | solution.py:95
  106.1 6.1 %collective-permute-start.17 = (f32[1,384,128]{2,1,0:T(8,128)S(1)}, f32[1,384,128]{2,1,0:T(8,128)S(1)}, u32[]{:S(2)}, u32[]{:S(2)}) collective-permute-start(f32[1,384,128]{2,1,0:T(8,128)S(1)} %slice_bitcast_fusion), channel_id=1, source_target_pairs={{0,2},{1,3},{2,0},{3,1},{4,6},{5,7},{6,4},{7,5},{8,10},{9,11},{10,... | collective-permute-start | bytes 589832 | tf_op jit(solution)/shard_map/ppermute | solution.py:95
  110.2 2.2 %collective-permute-start.7 = (f32[2,384,128]{2,1,0:T(8,128)S(1)}, f32[2,384,128]{2,1,0:T(8,128)S(1)}, u32[]{:S(2)}, u32[]{:S(2)}) collective-permute-start(f32[2,384,128]{2,1,0:T(8,128)S(1)} %maximum_bitcast_fusion.2.mine_ref.own_mine), channel_id=1, source_target_pairs={{0,1},{1,0},{2,3},{3,2},{4,5},{5,4},{6,7},{7,6},{8,9},{9,8},{10,11... | collective-permute-start | bytes 1179656 | tf_op jit(solution)/shard_map/ppermute | solution.py:95
  110.3 17.1 %collective-permute-start.19 = (f32[1,1152,128]{2,1,0:T(8,128)S(1)}, f32[1,1152,128]{2,1,0:T(8,128)S(1)}, u32[]{:S(2)}, u32[]{:S(2)}) collective-permute-start(f32[1,1152,128]{2,1,0:T(8,128)S(1)} %maximum_bitcast_fusion.1), channel_id=1, source_target_pairs={{0,2},{1,3},{2,0},{3,1},{4,6},{5,7},{6,4},{7,5},{8,10},{9,11},{10,... | collective-permute-start | bytes 1769480 | tf_op jit(solution)/shard_map/ppermute | solution.py:95
  112.3 15.8 %collective-permute-start.18 = (f32[2,384,128]{2,1,0:T(8,128)S(1)}, f32[2,384,128]{2,1,0:T(8,128)S(1)}, u32[]{:S(2)}, u32[]{:S(2)}) collective-permute-start(f32[2,384,128]{2,1,0:T(8,128)S(1)} %maximum_bitcast_fusion.3.late_mine), channel_id=1, source_target_pairs={{0,1},{1,0},{2,3},{3,2},{4,5},{5,4},{6,7},{7,6},{8,9},{9,8},{10,11... | collective-permute-start | bytes 1179656 | tf_op jit(solution)/shard_map/ppermute | solution.py:95
  127.6 20.1 %collective-permute-start.20 = (f32[2,1152,128]{2,1,0:T(8,128)S(1)}, f32[2,1152,128]{2,1,0:T(8,128)}, u32[]{:S(2)}, u32[]{:S(2)}) collective-permute-start(f32[2,1152,128]{2,1,0:T(8,128)S(1)} %maximum_bitcast_fusion.mine_ref), channel_id=1, source_target_pairs={{0,1},{1,0},{2,3},{3,2},{4,5},{5,4},{6,7},{7,6},{8,9},{9,8},{10,11... | collective-permute-start | bytes 3538952 | tf_op jit(solution)/shard_map/ppermute | solution.py:95
  (8 other events, 49.1 us)

commit v4 on v3

--- a/solution.py
+++ b/solution.py
@@ -161,7 +161,7 @@
     return copies
 
 
-def products_kernel(meta, keep, lo, total, with_sum, index_ref, blocks_ref, base_ref, applied_ref, *refs):
+def products_kernel(meta, keep, lo, total, with_sum, panels, index_ref, blocks_ref, base_ref, applied_ref, *refs):
     sums, refs = (refs[:1], refs[1:]) if with_sum else ((), refs)
     pieces, (out_ref, scratch, sem) = refs[: len(meta)], refs[len(meta) :]
     for copy in load_pieces(index_ref, keep, list(zip(meta, pieces)), lo, scratch, sem):
@@ -169,15 +169,16 @@
     depth = scratch.shape[1]
     chunk = min(512, depth)
     width = applied_ref.shape[0]
-    count = blocks_ref.shape[1]
+    count = (out_ref.shape[0] - panels * width) // LANES
+    own_blocks = (index_ref[0] & keep) * count
 
     def store(at, acc):
         acc = acc / total
         out_ref[at, :] = acc + sums[0][at, :] if with_sum else acc
 
     def block(i, _):
-        p = pl.multiple_of(blocks_ref[0, i] * LANES, LANES)
-        t = pl.multiple_of(blocks_ref[1, i] * LANES, LANES)
+        p = pl.multiple_of(blocks_ref[0, own_blocks + i] * LANES, LANES)
+        t = pl.multiple_of(blocks_ref[1, own_blocks + i] * LANES, LANES)
         acc = jnp.zeros((LANES, LANES), jnp.float32)
         for k in range(0, depth, chunk):
             acc += nt(scratch[pl.ds(p, LANES), k : k + chunk], scratch[pl.ds(t, LANES), k : k + chunk])
@@ -194,7 +195,7 @@
         store(pl.ds(pl.multiple_of(count * LANES + i * width, 8), width), acc)
         return 0
 
-    lax.fori_loop(0, (out_ref.shape[0] - count * LANES) // width, cross, 0)
+    lax.fori_loop(0, panels, cross, 0)
 
 
 def project_kernel(index_ref, inv_ref, mine_ref, other_ref, proj_ref, crosst):
@@ -305,10 +306,10 @@
     return pl.CostEstimate(flops=int(flops), bytes_accessed=int(moved), transcendentals=0)
 
 
-def share(blocks, parts, index):
+def share(blocks, parts):
     per = -(-len(blocks) // parts)
     table = jnp.array(blocks + blocks[-1:] * (per * parts - len(blocks)), jnp.int32).T
-    return per, lax.dynamic_slice_in_dim(table, index * per, per, 1)
+    return per, table
 
 
 def per_device(subspace, applied):
@@ -321,7 +322,7 @@
     n = size // 2 // LANES
     mode = lax.axis_index("modes")
     index = mode[None]
-    cut = depth // 2
+    cut = depth * 3 // 4
 
     near = [(0, 0, subspace)]
     far = []
@@ -338,23 +339,23 @@
     half_keep = modes // 2 - 1
     leading = side("modes", top) == 0
     own = [(p, t) for p in range(n) for t in range(p, n)]
-    per_own, own_share = share(own, modes // 2, mode & half_keep)
+    per_own, own_share = share(own, modes // 2)
     across = [(p, n + t) for p in range(n) for t in range(n)]
-    per_across, across_share = share(across, modes, mode)
-
-    def products(blocks, base, rows, keep, lo, span, pieces, sums=None):
+    per_across, across_share = share(across, modes)
+
+    def products(per, blocks, base, rows, keep, lo, span, pieces, sums=None):
         meta = tuple((mask, start) for mask, start, _ in pieces)
         given = [index, blocks, base, applied] + ([] if sums is None else [sums])
         return pl.pallas_call(
-            functools.partial(products_kernel, meta, keep, lo, total, sums is not None),
-            out_shape=jax.ShapeDtypeStruct((blocks.shape[1] * LANES + n * width, LANES), jnp.float32),
+            functools.partial(products_kernel, meta, keep, lo, total, sums is not None, n),
+            out_shape=jax.ShapeDtypeStruct((per * LANES + n * width, LANES), jnp.float32),
             in_specs=[smem] * 3 + [VMEM] * (len(given) - 3) + [ANY] * len(pieces),
             out_specs=VMEM,
             scratch_shapes=[pltpu.VMEM((rows, span), jnp.float32), pltpu.SemaphoreType.DMA((len(pieces),))],
             cost_estimate=cost(3e9, 4 * rows * span),
         )(*given, *[piece for _, _, piece in pieces])
 
-    early = products(own_share, jnp.zeros((1,), jnp.int32), size // 2, half_keep, 0, depth, near)
+    early = products(per_own, own_share, jnp.zeros((1,), jnp.int32), size // 2, half_keep, 0, depth, near)
     early = all_reduce_atoms(early)
     gram_own = gather_modes_pair(early[: per_own * LANES])
 
@@ -362,7 +363,7 @@
     late = None
     for held in far:
         lo, span = held[0][1], held[0][2].shape[1]
-        late = products(across_share, other_base, size, modes - 1, lo, span, near + held, late)
+        late = products(per_across, across_share, other_base, size, modes - 1, lo, span, near + held, late)
     late = all_reduce_atoms(late)
     gram_across = gather_modes_pair(late[: per_across * LANES])
     cross_own, cross_across = early[per_own * LANES :], late[per_across * LANES :]

time: 154 us -> 145 us (0.942)
  waiting for transfers between devices: 63 us -> 46.5 us
  starting transfers between devices: 20.6 us -> 25.2 us
  local copies, waits for them, and re-layouts: 7.61 us -> 10 us
    ppermute x21, waiting for transfers between devices: 63 us -> 46.5 us  [swap(): lax.ppermute(x, axis, [(i, i ^ 1 << bit) for i in range(lax.axis_size(axi...]
    ppermute x21, starting transfers between devices: 20.6 us -> 25.2 us  [swap(): lax.ppermute(x, axis, [(i, i ^ 1 << bit) for i in range(lax.axis_size(axi...]
    unnamed x22, local copies, waits for them, and re-layouts: 2.72 us -> 5.58 us
  transfers between devices with their start and end apart: 21 -> 21, of which waited for: 12 -> 9; matrix products, arithmetic and copies ran while one was open for 4% -> 4% of each run, Pallas kernels for 36% -> 38%
where the time goes in v4:
time: 145 us
  Pallas kernels  60.3 us (42%)
  waiting for transfers between devices  46.5 us (32%)
  starting transfers between devices  25.2 us (17%)
  local copies, waits for them, and re-layouts  10 us (7%)
  other arithmetic  1.61 us (1%)
    ppermute x21, waiting for transfers between devices, swap(): lax.ppermute(x, axis, [(i, i ^ 1 << bit) for i in range(lax.axis_size(axi...  46.5 us
    ppermute x21, starting transfers between devices, swap(): lax.ppermute(x, axis, [(i, i ^ 1 << bit) for i in range(lax.axis_size(axi...  25.2 us
    pallas_call x3, Pallas kernels, products(): pl.pallas_call(functools.partial(products_kernel, meta, keep, lo, total,...  21.7 us
    pallas_call x1, Pallas kernels, per_device(): second_call(index, first, *gram_own, *gram_across, *[piece for _, _, piec...  18.6 us
    pallas_call x1, Pallas kernels, per_device(): first = rest_call(first)  8.76 us
    pallas_call x1, Pallas kernels, per_device(): first = first_call(index, *gram_own)  5.67 us
    pallas_call x1, Pallas kernels, per_device(): pl.pallas_call(project_kernel, out_shape=jax.ShapeDtypeStruct((width, siz...  5.59 us
    unnamed x22, local copies, waits for them, and re-layouts  5.58 us
  transfers between devices with their start and end apart: 21, of which 9 were waited for; matrix products, arithmetic and copies ran while one was open for 4% of the time, Pallas kernels for 38%

profile of v4, /device:TPU:0, one launch (start us, length us, event | category | flops | bytes accessed | tf_op | source)
XLA Modules:
  0.0 144.5 jit_solution(16706878014792565075)
XLA Ops:
  2.5 2.6 %collective-permute-start.8 = (f32[192,1536]{1,0:T(8,128)S(1)}, f32[192,1536]{1,0:T(8,128)}, u32[]{:S(2)}, u32[]{:S(2)}) collective-permute-start(f32[192,1536]{1,0:T(8,128)S(1)} %slice.19), channel_id=1, source_target_pairs={{0,2},{1,3},{2,0},{3,1},{4,6},{5,7},{6,4},{7,5},{8,10},{9,11},{10,... | collective-permute-start | bytes 3538952 | tf_op jit(solution)/shard_map/ppermute | solution.py:95
  6.3 8.3 %shard_map.59 = f32[960,128]{1,0:T(8,128)} custom-call(s32[1]{0:T(128)} %bitcast.index_ref, s32[2,6]{1,0:T(2,128)} %constant.29.blocks_ref, s32[1]{0:T(128)} %constant.10.clone.1.base_ref, f32[192,2048]{1,0:T(8,128)} %applied_ref.5, f32[192,2048]{1,0:T(8,128)} %refs_0_.5, f32[192,2048]{1,0:T(8,128)} %copy-done.4), custom_call_target="tpu_custom_call" | custom-call | flops 3000000000 | bytes 3145728 | tf_op jit(solution)/shard_map/pallas_call | solution.py:349
  15.5 2.2 %collective-permute-start.1 = (f32[480,128]{1,0:T(8,128)S(1)}, f32[480,128]{1,0:T(8,128)S(1)}, u32[]{:S(2)}, u32[]{:S(2)}) collective-permute-start(f32[480,128]{1,0:T(8,128)S(1)} %constant_dynamic-slice_fusion.3), channel_id=1, source_target_pairs={{0,4},{4,0},{8,12},{12,8},{16,20},{20,16},{24,28},{28,24},{1,5},{5... | collective-permute-start | bytes 737288 | tf_op jit(solution)/shard_map/ppermute | solution.py:95
  17.7 14.1 %collective-permute-done.8.refs_2_ = f32[192,1536]{1,0:T(8,128)} collective-permute-done((f32[192,1536]{1,0:T(8,128)S(1)}, f32[192,1536]{1,0:T(8,128)}, u32[]{:S(2)}, u32[]{:S(2)}) %collective-permute-start.8) | collective-permute-done | bytes 1179680 | tf_op jit(solution)/shard_map/ppermute | solution.py:95
  32.9 1.9 %collective-permute-start.2 = (f32[240,128]{1,0:T(8,128)S(1)}, f32[240,128]{1,0:T(8,128)S(1)}, u32[]{:S(2)}, u32[]{:S(2)}) collective-permute-start(f32[240,128]{1,0:T(8,128)S(1)} %constant_dynamic-slice_fusion.2), channel_id=1, source_target_pairs={{0,8},{4,12},{8,0},{12,4},{16,24},{20,28},{24,16},{28,20},{1,9},{5... | collective-permute-start | bytes 368648 | tf_op jit(solution)/shard_map/ppermute | solution.py:95
  35.7 1.6 %collective-permute-start.10 = (f32[192,512]{1,0:T(8,128)S(1)}, f32[192,512]{1,0:T(8,128)S(1)}, u32[]{:S(2)}, u32[]{:S(2)}) collective-permute-start(f32[192,512]{1,0:T(8,128)S(1)} %slice.20), channel_id=1, source_target_pairs={{0,2},{1,3},{2,0},{3,1},{4,6},{5,7},{6,4},{7,5},{8,10},{9,11},{10,... | collective-permute-start | bytes 1179656 | tf_op jit(solution)/shard_map/ppermute | solution.py:95
  38.7 2.8 %collective-permute-start.3 = (f32[240,128]{1,0:T(8,128)S(1)}, f32[240,128]{1,0:T(8,128)S(1)}, u32[]{:S(2)}, u32[]{:S(2)}) collective-permute-start(f32[240,128]{1,0:T(8,128)S(1)} %dynamic-slice_add_fusion.3), channel_id=1, source_target_pairs={{0,16},{4,20},{8,24},{12,28},{16,0},{20,4},{24,8},{28,12},{1,17},{... | collective-permute-start | bytes 368648 | tf_op jit(solution)/shard_map/ppermute | solution.py:95
  41.6 5.8 %collective-permute-done.3 = f32[240,128]{1,0:T(8,128)S(1)} collective-permute-done((f32[240,128]{1,0:T(8,128)S(1)}, f32[240,128]{1,0:T(8,128)S(1)}, u32[]{:S(2)}, u32[]{:S(2)}) %collective-permute-start.3) | collective-permute-done | bytes 122912 | tf_op jit(solution)/shard_map/ppermute | solution.py:95
  48.1 4.1 %collective-permute-done.4 = f32[240,128]{1,0:T(8,128)S(1)} collective-permute-done((f32[240,128]{1,0:T(8,128)S(1)}, f32[240,128]{1,0:T(8,128)S(1)}, u32[]{:S(2)}, u32[]{:S(2)}) %collective-permute-start.4) | collective-permute-done | bytes 122912 | tf_op jit(solution)/shard_map/ppermute | solution.py:95
  52.3 1.6 %collective-permute-start.5 = (f32[480,128]{1,0:T(8,128)S(1)}, f32[480,128]{1,0:T(8,128)S(1)}, u32[]{:S(2)}, u32[]{:S(2)}) collective-permute-start(f32[480,128]{1,0:T(8,128)S(1)} %pad_maximum_fusion.2), channel_id=1, source_target_pairs={{0,4},{4,0},{8,12},{12,8},{16,20},{20,16},{24,28},{28,24},{1,5},{5... | collective-permute-start | bytes 737288 | tf_op jit(solution)/shard_map/ppermute | solution.py:95
  55.0 7.9 %shard_map.60.refs_0_ = f32[960,128]{1,0:T(8,128)} custom-call(s32[1]{0:T(128)} %bitcast.index_ref, s32[2,12]{1,0:T(2,128)} %constant.30.blocks_ref, s32[1]{0:T(128)} %bitcast.5.base_ref, f32[192,2048]{1,0:T(8,128)} %applied_ref.5, f32[192,2048]{1,0:T(8,128)} %refs_0_.5, f32[192,2048]{1,0:T(8,128)} %copy-done.4, f32[192,1536]{1,0:T(8,128)} %collective-permute-done.8.refs_2_, ...), custom_call_target="tpu_custom_call" | custom-call | flops 3000000000 | bytes 4718592 | tf_op jit(solution)/shard_map/pallas_call | solution.py:349
  63.7 5.5 %shard_map.61 = f32[960,128]{1,0:T(8,128)} custom-call(s32[1]{0:T(128)} %bitcast.index_ref, s32[2,12]{1,0:T(2,128)} %constant.30.blocks_ref, s32[1]{0:T(128)} %bitcast.5.base_ref, f32[192,2048]{1,0:T(8,128)} %applied_ref.5, f32[960,128]{1,0:T(8,128)} %shard_map.60.refs_0_, f32[192,2048]{1,0:T(8,128)} %refs_0_.5, f32[192,2048]{1,0:T(8,128)} %copy-done.4, ...), custom_call_target="tpu_custom_call" | custom-call | flops 3000000000 | bytes 1572864 | tf_op jit(solution)/shard_map/pallas_call | solution.py:349
  70.9 5.7 %collective-permute-done.12 = f32[480,128]{1,0:T(8,128)S(1)} collective-permute-done((f32[480,128]{1,0:T(8,128)S(1)}, f32[480,128]{1,0:T(8,128)S(1)}, u32[]{:S(2)}, u32[]{:S(2)}) %collective-permute-start.12) | collective-permute-done | bytes 245792 | tf_op jit(solution)/shard_map/ppermute | solution.py:95
  76.6 1.7 %collective-permute-start.13 = (f32[240,128]{1,0:T(8,128)S(1)}, f32[240,128]{1,0:T(8,128)S(1)}, u32[]{:S(2)}, u32[]{:S(2)}) collective-permute-start(f32[240,128]{1,0:T(8,128)S(1)} %constant_dynamic-slice_fusion), channel_id=1, source_target_pairs={{0,8},{4,12},{8,0},{12,4},{16,24},{20,28},{24,16},{28,20},{1,9},{5... | collective-permute-start | bytes 368648 | tf_op jit(solution)/shard_map/ppermute | solution.py:95
  79.8 1.7 %collective-permute-done.13 = f32[240,128]{1,0:T(8,128)S(1)} collective-permute-done((f32[240,128]{1,0:T(8,128)S(1)}, f32[240,128]{1,0:T(8,128)S(1)}, u32[]{:S(2)}, u32[]{:S(2)}) %collective-permute-start.13) | collective-permute-done | bytes 122912 | tf_op jit(solution)/shard_map/ppermute | solution.py:95
  81.5 4.3 %collective-permute-start.14 = (f32[240,128]{1,0:T(8,128)S(1)}, f32[240,128]{1,0:T(8,128)S(1)}, u32[]{:S(2)}, u32[]{:S(2)}) collective-permute-start(f32[240,128]{1,0:T(8,128)S(1)} %dynamic-slice_add_fusion.2), channel_id=1, source_target_pairs={{0,16},{4,20},{8,24},{12,28},{16,0},{20,4},{24,8},{28,12},{1,17},{... | collective-permute-start | bytes 368648 | tf_op jit(solution)/shard_map/ppermute | solution.py:95
  85.9 4.1 %collective-permute-done.14 = f32[240,128]{1,0:T(8,128)S(1)} collective-permute-done((f32[240,128]{1,0:T(8,128)S(1)}, f32[240,128]{1,0:T(8,128)S(1)}, u32[]{:S(2)}, u32[]{:S(2)}) %collective-permute-start.14) | collective-permute-done | bytes 122912 | tf_op jit(solution)/shard_map/ppermute | solution.py:95
  90.3 4.7 %collective-permute-done.15 = f32[240,128]{1,0:T(8,128)S(1)} collective-permute-done((f32[240,128]{1,0:T(8,128)S(1)}, f32[240,128]{1,0:T(8,128)S(1)}, u32[]{:S(2)}, u32[]{:S(2)}) %collective-permute-start.15) | collective-permute-done | bytes 122912 | tf_op jit(solution)/shard_map/ppermute | solution.py:95
  96.4 5.7 %inverse_first.1.held_ref = f32[384,384]{1,0:T(8,128)} custom-call(s32[1]{0:T(128)} %bitcast.index_ref, f32[2,384,128]{2,1,0:T(8,128)} %copy-done.2, f32[2,384,128]{2,1,0:T(8,128)} %copy-done.9), custom_call_target="tpu_custom_call" | custom-call | flops 5000000000 | bytes 1000000 | tf_op jit(solution)/shard_map/inverse_first/pallas_call | solution.py:383
  102.1 1.6 %collective-permute-start.17 = (f32[1,384,128]{2,1,0:T(8,128)S(1)}, f32[1,384,128]{2,1,0:T(8,128)S(1)}, u32[]{:S(2)}, u32[]{:S(2)}) collective-permute-start(f32[1,384,128]{2,1,0:T(8,128)S(1)} %slice_bitcast_fusion), channel_id=1, source_target_pairs={{0,2},{1,3},{2,0},{3,1},{4,6},{5,7},{6,4},{7,5},{8,10},{9,11},{10,... | collective-permute-start | bytes 589832 | tf_op jit(solution)/shard_map/ppermute | solution.py:95
  104.4 8.8 %inverse_rest.1.first_ref = f32[384,384]{1,0:T(8,128)} custom-call(f32[384,384]{1,0:T(8,128)} %inverse_first.1.held_ref), custom_call_target="tpu_custom_call" | custom-call | flops 10000000000 | bytes 1000000 | tf_op jit(solution)/shard_map/inverse_rest/pallas_call | solution.py:392
  113.3 4.8 %collective-permute-done.19 = f32[1,1152,128]{2,1,0:T(8,128)S(1)} collective-permute-done((f32[1,1152,128]{2,1,0:T(8,128)S(1)}, f32[1,1152,128]{2,1,0:T(8,128)S(1)}, u32[]{:S(2)}, u32[]{:S(2)}) %collective-permute-start.19) | collective-permute-done | bytes 589856 | tf_op jit(solution)/shard_map/ppermute | solution.py:95
  119.2 18.6 %inverse_second.1 = (f32[768,768]{1,0:T(8,128)}, f32[192,2048]{1,0:T(8,128)}) custom-call(s32[1]{0:T(128)} %bitcast.index_ref, f32[384,384]{1,0:T(8,128)} %inverse_rest.1.first_ref, f32[2,384,128]{2,1,0:T(8,128)} %copy-done.2, f32[2,384,128]{2,1,0:T(8,128)} %copy-done.9, f32[2,384,128]{2,1,0:T(8,128)} %copy-done.3, f32[2,384,128]{2,1,0:T(8,128)} %copy-done.10, ...), custom_call_target="tpu_custom_call" | custom-call | flops 20000000000 | bytes 8000000 | tf_op jit(solution)/shard_map/inverse_second/pallas_call | solution.py:413
  138.9 5.6 %project.1 = f32[192,768]{1,0:T(8,128)} custom-call(s32[1]{0:T(128)} %bitcast.index_ref, f32[768,768]{1,0:T(8,128)} %get-tuple-element.5.inv_ref, f32[2,1152,128]{2,1,0:T(8,128)} %copy-done, f32[2,1152,128]{2,1,0:T(8,128)} %copy-done.6), custom_call_target="tpu_custom_call" | custom-call | flops 2000000000 | bytes 5000000 | tf_op jit(solution)/shard_map/project/pallas_call | solution.py:414
  (75 shorter events, 18.0 us)
Async XLA Ops:
  0.6 4.5 %collective-permute-start = (f32[192,2048]{1,0:T(8,128)}, f32[192,2048]{1,0:T(8,128)S(1)}, u32[]{:S(2)}, u32[]{:S(2)}) collective-permute-start(f32[192,2048]{1,0:T(8,128)} %refs_0_.5), channel_id=1, source_target_pairs={{0,1},{1,0},{2,3},{3,2},{4,5},{5,4},{6,7},{7,6},{8,9},{9,8},{10,11... | collective-permute-start | bytes 4718600 | tf_op jit(solution)/shard_map/ppermute | solution.py:95
  2.5 29.3 %collective-permute-start.8 = (f32[192,1536]{1,0:T(8,128)S(1)}, f32[192,1536]{1,0:T(8,128)}, u32[]{:S(2)}, u32[]{:S(2)}) collective-permute-start(f32[192,1536]{1,0:T(8,128)S(1)} %slice.19), channel_id=1, source_target_pairs={{0,2},{1,3},{2,0},{3,1},{4,6},{5,7},{6,4},{7,5},{8,10},{9,11},{10,... | collective-permute-start | bytes 3538952 | tf_op jit(solution)/shard_map/ppermute | solution.py:95
  15.5 16.3 %collective-permute-start.1 = (f32[480,128]{1,0:T(8,128)S(1)}, f32[480,128]{1,0:T(8,128)S(1)}, u32[]{:S(2)}, u32[]{:S(2)}) collective-permute-start(f32[480,128]{1,0:T(8,128)S(1)} %constant_dynamic-slice_fusion.3), channel_id=1, source_target_pairs={{0,4},{4,0},{8,12},{12,8},{16,20},{20,16},{24,28},{28,24},{1,5},{5... | collective-permute-start | bytes 737288 | tf_op jit(solution)/shard_map/ppermute | solution.py:95
  31.9 22.1 %collective-permute-start.9 = (f32[192,1536]{1,0:T(8,128)}, f32[192,1536]{1,0:T(8,128)S(1)}, u32[]{:S(2)}, u32[]{:S(2)}) collective-permute-start(f32[192,1536]{1,0:T(8,128)} %collective-permute-done.8.refs_2_), channel_id=1, source_target_pairs={{0,1},{1,0},{2,3},{3,2},{4,5},{5,4},{6,7},{7,6},{8,9},{9,8},{10,11... | collective-permute-start | bytes 3538952 | tf_op jit(solution)/shard_map/ppermute | solution.py:95
  32.9 5.9 %collective-permute-start.2 = (f32[240,128]{1,0:T(8,128)S(1)}, f32[240,128]{1,0:T(8,128)S(1)}, u32[]{:S(2)}, u32[]{:S(2)}) collective-permute-start(f32[240,128]{1,0:T(8,128)S(1)} %constant_dynamic-slice_fusion.2), channel_id=1, source_target_pairs={{0,8},{4,12},{8,0},{12,4},{16,24},{20,28},{24,16},{28,20},{1,9},{5... | collective-permute-start | bytes 368648 | tf_op jit(solution)/shard_map/ppermute | solution.py:95
  35.7 12.4 %collective-permute-start.10 = (f32[192,512]{1,0:T(8,128)S(1)}, f32[192,512]{1,0:T(8,128)S(1)}, u32[]{:S(2)}, u32[]{:S(2)}) collective-permute-start(f32[192,512]{1,0:T(8,128)S(1)} %slice.20), channel_id=1, source_target_pairs={{0,2},{1,3},{2,0},{3,1},{4,6},{5,7},{6,4},{7,5},{8,10},{9,11},{10,... | collective-permute-start | bytes 1179656 | tf_op jit(solution)/shard_map/ppermute | solution.py:95
  38.7 8.6 %collective-permute-start.3 = (f32[240,128]{1,0:T(8,128)S(1)}, f32[240,128]{1,0:T(8,128)S(1)}, u32[]{:S(2)}, u32[]{:S(2)}) collective-permute-start(f32[240,128]{1,0:T(8,128)S(1)} %dynamic-slice_add_fusion.3), channel_id=1, source_target_pairs={{0,16},{4,20},{8,24},{12,28},{16,0},{20,4},{24,8},{28,12},{1,17},{... | collective-permute-start | bytes 368648 | tf_op jit(solution)/shard_map/ppermute | solution.py:95
  47.3 4.9 %collective-permute-start.4 = (f32[240,128]{1,0:T(8,128)S(1)}, f32[240,128]{1,0:T(8,128)S(1)}, u32[]{:S(2)}, u32[]{:S(2)}) collective-permute-start(f32[240,128]{1,0:T(8,128)S(1)} %add.40), channel_id=1, source_target_pairs={{0,8},{4,12},{8,0},{12,4},{16,24},{20,28},{24,16},{28,20},{1,9},{5... | collective-permute-start | bytes 368648 | tf_op jit(solution)/shard_map/ppermute | solution.py:95
  48.1 14.8 %copy-start.7 = (f32[192,512]{1,0:T(8,128)}, f32[192,512]{1,0:T(8,128)S(1)}, u32[]{:S(2)}) copy-start(f32[192,512]{1,0:T(8,128)S(1)} %collective-permute-done.10.refs_3_.refs_4_) | copy-start | bytes 1179652
  48.1 14.8 %collective-permute-start.11 = (f32[192,512]{1,0:T(8,128)S(1)}, f32[192,512]{1,0:T(8,128)S(1)}, u32[]{:S(2)}, u32[]{:S(2)}) collective-permute-start(f32[192,512]{1,0:T(8,128)S(1)} %collective-permute-done.10.refs_3_.refs_4_), channel_id=1, source_target_pairs={{0,1},{1,0},{2,3},{3,2},{4,5},{5,4},{6,7},{7,6},{8,9},{9,8},{10,11... | collective-permute-start | bytes 1179656 | tf_op jit(solution)/shard_map/ppermute | solution.py:95
  52.3 18.5 %collective-permute-start.5 = (f32[480,128]{1,0:T(8,128)S(1)}, f32[480,128]{1,0:T(8,128)S(1)}, u32[]{:S(2)}, u32[]{:S(2)}) collective-permute-start(f32[480,128]{1,0:T(8,128)S(1)} %pad_maximum_fusion.2), channel_id=1, source_target_pairs={{0,4},{4,0},{8,12},{12,8},{16,20},{20,16},{24,28},{28,24},{1,5},{5... | collective-permute-start | bytes 737288 | tf_op jit(solution)/shard_map/ppermute | solution.py:95
  69.2 7.3 %copy-start.1 = (f32[960,128]{1,0:T(8,128)S(1)}, f32[960,128]{1,0:T(8,128)}, u32[]{:S(2)}) copy-start(f32[960,128]{1,0:T(8,128)} %shard_map.61) | copy-start | bytes 1474564
  70.3 6.3 %collective-permute-start.12 = (f32[480,128]{1,0:T(8,128)S(1)}, f32[480,128]{1,0:T(8,128)S(1)}, u32[]{:S(2)}, u32[]{:S(2)}) collective-permute-start(f32[480,128]{1,0:T(8,128)S(1)} %constant_dynamic-slice_fusion.1), channel_id=1, source_target_pairs={{0,4},{4,0},{8,12},{12,8},{16,20},{20,16},{24,28},{28,24},{1,5},{5... | collective-permute-start | bytes 737288 | tf_op jit(solution)/shard_map/ppermute | solution.py:95
  76.6 4.9 %collective-permute-start.13 = (f32[240,128]{1,0:T(8,128)S(1)}, f32[240,128]{1,0:T(8,128)S(1)}, u32[]{:S(2)}, u32[]{:S(2)}) collective-permute-start(f32[240,128]{1,0:T(8,128)S(1)} %constant_dynamic-slice_fusion), channel_id=1, source_target_pairs={{0,8},{4,12},{8,0},{12,4},{16,24},{20,28},{24,16},{28,20},{1,9},{5... | collective-permute-start | bytes 368648 | tf_op jit(solution)/shard_map/ppermute | solution.py:95
  78.3 7.6 %collective-permute-start.6 = (f32[1,384,128]{2,1,0:T(8,128)S(1)}, f32[1,384,128]{2,1,0:T(8,128)S(1)}, u32[]{:S(2)}, u32[]{:S(2)}) collective-permute-start(f32[1,384,128]{2,1,0:T(8,128)S(1)} %slice_bitcast_fusion.1), channel_id=1, source_target_pairs={{0,2},{1,3},{2,0},{3,1},{4,6},{5,7},{6,4},{7,5},{8,10},{9,11},{10,... | collective-permute-start | bytes 589832 | tf_op jit(solution)/shard_map/ppermute | solution.py:95
  81.5 8.5 %collective-permute-start.14 = (f32[240,128]{1,0:T(8,128)S(1)}, f32[240,128]{1,0:T(8,128)S(1)}, u32[]{:S(2)}, u32[]{:S(2)}) collective-permute-start(f32[240,128]{1,0:T(8,128)S(1)} %dynamic-slice_add_fusion.2), channel_id=1, source_target_pairs={{0,16},{4,20},{8,24},{12,28},{16,0},{20,4},{24,8},{28,12},{1,17},{... | collective-permute-start | bytes 368648 | tf_op jit(solution)/shard_map/ppermute | solution.py:95
  90.1 4.9 %collective-permute-start.15 = (f32[240,128]{1,0:T(8,128)S(1)}, f32[240,128]{1,0:T(8,128)S(1)}, u32[]{:S(2)}, u32[]{:S(2)}) collective-permute-start(f32[240,128]{1,0:T(8,128)S(1)} %add.43), channel_id=1, source_target_pairs={{0,8},{4,12},{8,0},{12,4},{16,24},{20,28},{24,16},{28,20},{1,9},{5... | collective-permute-start | bytes 368648 | tf_op jit(solution)/shard_map/ppermute | solution.py:95
  90.2 5.5 %collective-permute-start.7 = (f32[2,384,128]{2,1,0:T(8,128)S(1)}, f32[2,384,128]{2,1,0:T(8,128)S(1)}, u32[]{:S(2)}, u32[]{:S(2)}) collective-permute-start(f32[2,384,128]{2,1,0:T(8,128)S(1)} %maximum_bitcast_fusion.2.mine_ref.own_mine), channel_id=1, source_target_pairs={{0,1},{1,0},{2,3},{3,2},{4,5},{5,4},{6,7},{7,6},{8,9},{9,8},{10,11... | collective-permute-start | bytes 1179656 | tf_op jit(solution)/shard_map/ppermute | solution.py:95
  95.0 7.0 %collective-permute-start.16 = (f32[480,128]{1,0:T(8,128)S(1)}, f32[480,128]{1,0:T(8,128)S(1)}, u32[]{:S(2)}, u32[]{:S(2)}) collective-permute-start(f32[480,128]{1,0:T(8,128)S(1)} %pad_maximum_fusion.3), channel_id=1, source_target_pairs={{0,4},{4,0},{8,12},{12,8},{16,20},{20,16},{24,28},{28,24},{1,5},{5... | collective-permute-start | bytes 737288 | tf_op jit(solution)/shard_map/ppermute | solution.py:95
  102.1 11.0 %collective-permute-start.17 = (f32[1,384,128]{2,1,0:T(8,128)S(1)}, f32[1,384,128]{2,1,0:T(8,128)S(1)}, u32[]{:S(2)}, u32[]{:S(2)}) collective-permute-start(f32[1,384,128]{2,1,0:T(8,128)S(1)} %slice_bitcast_fusion), channel_id=1, source_target_pairs={{0,2},{1,3},{2,0},{3,1},{4,6},{5,7},{6,4},{7,5},{8,10},{9,11},{10,... | collective-permute-start | bytes 589832 | tf_op jit(solution)/shard_map/ppermute | solution.py:95
  103.8 14.3 %collective-permute-start.19 = (f32[1,1152,128]{2,1,0:T(8,128)S(1)}, f32[1,1152,128]{2,1,0:T(8,128)S(1)}, u32[]{:S(2)}, u32[]{:S(2)}) collective-permute-start(f32[1,1152,128]{2,1,0:T(8,128)S(1)} %maximum_bitcast_fusion.1), channel_id=1, source_target_pairs={{0,2},{1,3},{2,0},{3,1},{4,6},{5,7},{6,4},{7,5},{8,10},{9,11},{10,... | collective-permute-start | bytes 1769480 | tf_op jit(solution)/shard_map/ppermute | solution.py:95
  113.3 5.1 %collective-permute-start.18 = (f32[2,384,128]{2,1,0:T(8,128)S(1)}, f32[2,384,128]{2,1,0:T(8,128)S(1)}, u32[]{:S(2)}, u32[]{:S(2)}) collective-permute-start(f32[2,384,128]{2,1,0:T(8,128)S(1)} %maximum_bitcast_fusion.3.late_mine), channel_id=1, source_target_pairs={{0,1},{1,0},{2,3},{3,2},{4,5},{5,4},{6,7},{7,6},{8,9},{9,8},{10,11... | collective-permute-start | bytes 1179656 | tf_op jit(solution)/shard_map/ppermute | solution.py:95
  118.3 19.6 %copy-start = (f32[2,1152,128]{2,1,0:T(8,128)}, f32[2,1152,128]{2,1,0:T(8,128)S(1)}, u32[]{:S(2)}) copy-start(f32[2,1152,128]{2,1,0:T(8,128)S(1)} %maximum_bitcast_fusion.mine_ref) | copy-start | bytes 3538948
  118.3 19.6 %collective-permute-start.20 = (f32[2,1152,128]{2,1,0:T(8,128)S(1)}, f32[2,1152,128]{2,1,0:T(8,128)S(1)}, u32[]{:S(2)}, u32[]{:S(2)}) collective-permute-start(f32[2,1152,128]{2,1,0:T(8,128)S(1)} %maximum_bitcast_fusion.mine_ref), channel_id=1, source_target_pairs={{0,1},{1,0},{2,3},{3,2},{4,5},{5,4},{6,7},{7,6},{8,9},{9,8},{10,11... | collective-permute-start | bytes 3538952 | tf_op jit(solution)/shard_map/ppermute | solution.py:95
  (8 other events, 16.0 us)
